TPU v7x, 128 devices: a whole 4x4x4 slice. The times are simulated.
128 devices in a mesh: dp: 1, cols: 16 (over z, y), rows: 8 (over x, core).
Axes of the slice: x: 4, y: 4, z: 4, core: 2. Of those that a mesh axis runs over, the one named last changes fastest.
Arguments:
- frames: bfloat16 [16, 1, 256, 512, 64], P(None, 'dp', 'rows', 'cols')
- w_in: bfloat16 [3, 3, 64, 768], replicated
- w_rec: bfloat16 [3, 3, 192, 768], replicated
- gate_bias: float32 [768], replicated
- h_init: bfloat16 [1, 256, 512, 192], P('dp', 'rows', 'cols')
- c_init: float32 [1, 256, 512, 192], P('dp', 'rows', 'cols')
Outputs:
- output 1: bfloat16 [16, 1, 256, 512, 192], P(None, 'dp', 'rows', 'cols')
- output 2: float32 [1, 256, 512, 192], P('dp', 'rows', 'cols')
All inputs are finite; a program needn't handle non-finite values.
Results may differ from a plain program's by a relative error of at most 0.00385845.
Values are sent between devices in bfloat16 or wider.
A program may use at most 1 GiB of HBM per device.

v0:
```python
import jax
import jax.numpy as jnp
from jax import lax
from jax.sharding import PartitionSpec as P, NamedSharding

CONV_DIMS = ("NHWC", "HWIO", "NHWC")


def conv_valid(operand, kernel):
    return lax.conv_general_dilated(operand, kernel, (1, 1), "VALID", dimension_numbers=CONV_DIMS, preferred_element_type=jnp.float32)


def cell_update(gate_pre, c_prev):
    gate_i, gate_f, gate_o, gate_g = jnp.split(gate_pre, 4, axis=-1)
    c_next = jax.nn.sigmoid(gate_f) * c_prev + jax.nn.sigmoid(gate_i) * jnp.tanh(gate_g)
    h_next = (jax.nn.sigmoid(gate_o) * jnp.tanh(c_next)).astype(jnp.bfloat16)
    return h_next, c_next


def edge_exchange(tile_in, axis_name, axis_size, axis_dim, width):
    length = tile_in.shape[axis_dim]
    low_part = lax.slice_in_dim(tile_in, 0, width, axis=axis_dim)
    high_part = lax.slice_in_dim(tile_in, length - width, length, axis=axis_dim)
    if axis_size == 1:
        from_prev = jnp.zeros_like(high_part)
        from_next = jnp.zeros_like(low_part)
    else:
        forward = [(source, source + 1) for source in range(axis_size - 1)]
        backward = [(source + 1, source) for source in range(axis_size - 1)]
        from_prev = lax.ppermute(high_part, axis_name, forward)
        from_next = lax.ppermute(low_part, axis_name, backward)
    return jnp.concatenate([from_prev, tile_in, from_next], axis=axis_dim)


def add_halo(tile_in, width, n_rows, n_cols):
    row_dim = tile_in.ndim - 3
    tall_tile = edge_exchange(tile_in, "rows", n_rows, row_dim, width)
    return edge_exchange(tall_tile, "cols", n_cols, row_dim + 1, width)


def solution(mesh):
    n_rows = mesh.shape["rows"]
    n_cols = mesh.shape["cols"]
    seq_spec = P(None, "dp", "rows", "cols", None)
    state_spec = P("dp", "rows", "cols", None)

    def local_run(frames, w_in, w_rec, gate_bias, h_init, c_init):
        frames_ext = add_halo(frames, 1, n_rows, n_cols)

        def time_step(carry_in, frame_ext):
            h_prev, c_prev = carry_in
            h_ext = add_halo(h_prev, 1, n_rows, n_cols)
            gate_pre = conv_valid(frame_ext, w_in) + conv_valid(h_ext, w_rec) + gate_bias
            h_next, c_next = cell_update(gate_pre, c_prev)
            return (h_next, c_next), h_next

        (h_last, c_last), hidden_seq = lax.scan(time_step, (h_init, c_init), frames_ext)
        return hidden_seq, c_last

    return jax.shard_map(local_run, mesh=mesh, in_specs=(seq_spec, P(), P(), P(), state_spec, state_spec), out_specs=(seq_spec, state_spec), check_vma=False)
```

profile of v0, /device:TPU:97, one launch (start us, length us, event | category | flops | bytes accessed | tf_op | source)
XLA Modules:
  0.0 534.0 jit_solution(15820924194910731039)
XLA Ops:
  26.6 6.5 %pad_maximum_fusion.3 = bf16[16,1,34,34,64]{4,2,3,1,0:T(8,128)(2,1)} fusion(bf16[16,1,34,1,64]{4,2,3,1,0:T(8,128)(2,1)} %collective-permute-done.7, bf16[16,1,1,32,64]{4,2,3,1,0:T(2,128)(2,1)S(1)} %collective-permute-done.5, bf16[16,1,32,32,64]{4,2,3,1,0:T(8,128)(2,1)} %copy-done, bf16[16,1,1,32,64]{4,2,3,1,0:T(2,128)(2,1)S(1)} %collective-permute-done.4, ...), kind=kLoop, calls=%fused_computation.51 | loop fusion | flops 11837440 | bytes 4734976 | tf_op jit(solution)/shard_map/concatenate | solution.py:32
  33.2 499.2 %while.14 = (s32[]{:T(128)}, bf16[1,32,32,192]{3,1,2,0:T(8,128)(2,1)S(1)}, f32[1,32,32,192]{3,1,2,0:T(8,128)S(1)}, bf16[16,1,32,32,192]{4,3,2,1,0:T(8,128)(2,1)}...) while((s32[]{:T(128)}, ...), condition=%wide.region_1.2_spmd, body=%wide.region_0.1_spmd.sunk | while | flops 4542246912 | bytes 49965924 | solution.py:57
  40.5 6.2 %collective-permute-start.2 = (bf16[1,34,1,192]{3,1,2,0:T(8,128)(2,1)S(1)}, bf16[1,34,1,192]{3,1,2,0:T(8,128)(2,1)S(1)}, u32[]{:S(2)}, u32[]{:S(2)}) collective-permute-start(bf16[1,34,1,192]{3,1,2,0:T(8,128)(2,1)S(1)} %get-tuple-element.146), channel_id=1, source_target_pairs={{8,0},{16,8},{24,16},{32,24},{40,32},{48,40},{56,48},{64,56},{72,6... | collective-permute-start | bytes 39176 | tf_op jit(solution)/shard_map/while/body/eval_jaxpr/ppermute | solution.py:31
  54.2 6.2 %add_add_fusion.2 = f32[32,8,5,768]{3,1,2,0:T(8,128)S(1)} fusion(f32[32,8,5,768]{3,1,2,0:T(8,128)} %fusion.54, f32[768]{0:T(1024)S(1)} %get-tuple-element.182, pred[8,5]{0,1:T(8,128)(4,1)S(1)} %get-tuple-element.185, bf16[3,3,192,768]{3,2,1,0:T(8,128)(2,1)S(1)} %copy-done.3, bf16[34,1,7,2,192]{4,2,3,0,1:T(8,128)(2,1)S(1)} %slice.104, ...), kind=kOutput, calls=%fused_computation.clone.1 | convolution fusion | flops 3403511808 | bytes 11226664 | tf_op jit(solution)/shard_map/while/body/eval_jaxpr/conv_general_dilated | solution.py:10
  66.6 5.4 %collective-permute-start.1 = (bf16[1,1,32,192]{3,1,2,0:T(2,128)(2,1)S(1)}, bf16[1,1,32,192]{3,1,2,0:T(2,128)(2,1)S(1)}, u32[]{:S(2)}, u32[]{:S(2)}) collective-permute-start(bf16[1,1,32,192]{3,1,2,0:T(2,128)(2,1)S(1)} %get-tuple-element.145), channel_id=1, source_target_pairs={{0,1},{1,2},{2,3},{3,4},{4,5},{5,6},{6,7},{8,9},{9,10},{10,11},{11... | collective-permute-start | bytes 36872 | tf_op jit(solution)/shard_map/while/body/eval_jaxpr/ppermute | solution.py:30
  85.3 6.2 %add_add_fusion.2 = f32[32,8,5,768]{3,1,2,0:T(8,128)S(1)} fusion(f32[32,8,5,768]{3,1,2,0:T(8,128)} %fusion.54, f32[768]{0:T(1024)S(1)} %get-tuple-element.182, pred[8,5]{0,1:T(8,128)(4,1)S(1)} %get-tuple-element.185, bf16[3,3,192,768]{3,2,1,0:T(8,128)(2,1)S(1)} %copy-done.3, bf16[34,1,7,2,192]{4,2,3,0,1:T(8,128)(2,1)S(1)} %slice.104, ...), kind=kOutput, calls=%fused_computation.clone.1 | convolution fusion | flops 3403511808 | bytes 11226664 | tf_op jit(solution)/shard_map/while/body/eval_jaxpr/conv_general_dilated | solution.py:10
  97.8 5.4 %collective-permute-start.1 = (bf16[1,1,32,192]{3,1,2,0:T(2,128)(2,1)S(1)}, bf16[1,1,32,192]{3,1,2,0:T(2,128)(2,1)S(1)}, u32[]{:S(2)}, u32[]{:S(2)}) collective-permute-start(bf16[1,1,32,192]{3,1,2,0:T(2,128)(2,1)S(1)} %get-tuple-element.145), channel_id=1, source_target_pairs={{0,1},{1,2},{2,3},{3,4},{4,5},{5,6},{6,7},{8,9},{9,10},{10,11},{11... | collective-permute-start | bytes 36872 | tf_op jit(solution)/shard_map/while/body/eval_jaxpr/ppermute | solution.py:30
  104.5 4.6 collective-permute-start.2
  116.5 6.2 %add_add_fusion.2 = f32[32,8,5,768]{3,1,2,0:T(8,128)S(1)} fusion(f32[32,8,5,768]{3,1,2,0:T(8,128)} %fusion.54, f32[768]{0:T(1024)S(1)} %get-tuple-element.182, pred[8,5]{0,1:T(8,128)(4,1)S(1)} %get-tuple-element.185, bf16[3,3,192,768]{3,2,1,0:T(8,128)(2,1)S(1)} %copy-done.3, bf16[34,1,7,2,192]{4,2,3,0,1:T(8,128)(2,1)S(1)} %slice.104, ...), kind=kOutput, calls=%fused_computation.clone.1 | convolution fusion | flops 3403511808 | bytes 11226664 | tf_op jit(solution)/shard_map/while/body/eval_jaxpr/conv_general_dilated | solution.py:10
  129.0 5.4 %collective-permute-start.1 = (bf16[1,1,32,192]{3,1,2,0:T(2,128)(2,1)S(1)}, bf16[1,1,32,192]{3,1,2,0:T(2,128)(2,1)S(1)}, u32[]{:S(2)}, u32[]{:S(2)}) collective-permute-start(bf16[1,1,32,192]{3,1,2,0:T(2,128)(2,1)S(1)} %get-tuple-element.145), channel_id=1, source_target_pairs={{0,1},{1,2},{2,3},{3,4},{4,5},{5,6},{6,7},{8,9},{9,10},{10,11},{11... | collective-permute-start | bytes 36872 | tf_op jit(solution)/shard_map/while/body/eval_jaxpr/ppermute | solution.py:30
  135.7 4.6 collective-permute-start.2
  147.7 6.2 %add_add_fusion.2 = f32[32,8,5,768]{3,1,2,0:T(8,128)S(1)} fusion(f32[32,8,5,768]{3,1,2,0:T(8,128)} %fusion.54, f32[768]{0:T(1024)S(1)} %get-tuple-element.182, pred[8,5]{0,1:T(8,128)(4,1)S(1)} %get-tuple-element.185, bf16[3,3,192,768]{3,2,1,0:T(8,128)(2,1)S(1)} %copy-done.3, bf16[34,1,7,2,192]{4,2,3,0,1:T(8,128)(2,1)S(1)} %slice.104, ...), kind=kOutput, calls=%fused_computation.clone.1 | convolution fusion | flops 3403511808 | bytes 11226664 | tf_op jit(solution)/shard_map/while/body/eval_jaxpr/conv_general_dilated | solution.py:10
  160.2 5.4 %collective-permute-start.1 = (bf16[1,1,32,192]{3,1,2,0:T(2,128)(2,1)S(1)}, bf16[1,1,32,192]{3,1,2,0:T(2,128)(2,1)S(1)}, u32[]{:S(2)}, u32[]{:S(2)}) collective-permute-start(bf16[1,1,32,192]{3,1,2,0:T(2,128)(2,1)S(1)} %get-tuple-element.145), channel_id=1, source_target_pairs={{0,1},{1,2},{2,3},{3,4},{4,5},{5,6},{6,7},{8,9},{9,10},{10,11},{11... | collective-permute-start | bytes 36872 | tf_op jit(solution)/shard_map/while/body/eval_jaxpr/ppermute | solution.py:30
  166.8 4.6 collective-permute-start.2
  178.9 6.2 %add_add_fusion.2 = f32[32,8,5,768]{3,1,2,0:T(8,128)S(1)} fusion(f32[32,8,5,768]{3,1,2,0:T(8,128)} %fusion.54, f32[768]{0:T(1024)S(1)} %get-tuple-element.182, pred[8,5]{0,1:T(8,128)(4,1)S(1)} %get-tuple-element.185, bf16[3,3,192,768]{3,2,1,0:T(8,128)(2,1)S(1)} %copy-done.3, bf16[34,1,7,2,192]{4,2,3,0,1:T(8,128)(2,1)S(1)} %slice.104, ...), kind=kOutput, calls=%fused_computation.clone.1 | convolution fusion | flops 3403511808 | bytes 11226664 | tf_op jit(solution)/shard_map/while/body/eval_jaxpr/conv_general_dilated | solution.py:10
  191.4 5.4 %collective-permute-start.1 = (bf16[1,1,32,192]{3,1,2,0:T(2,128)(2,1)S(1)}, bf16[1,1,32,192]{3,1,2,0:T(2,128)(2,1)S(1)}, u32[]{:S(2)}, u32[]{:S(2)}) collective-permute-start(bf16[1,1,32,192]{3,1,2,0:T(2,128)(2,1)S(1)} %get-tuple-element.145), channel_id=1, source_target_pairs={{0,1},{1,2},{2,3},{3,4},{4,5},{5,6},{6,7},{8,9},{9,10},{10,11},{11... | collective-permute-start | bytes 36872 | tf_op jit(solution)/shard_map/while/body/eval_jaxpr/ppermute | solution.py:30
  198.0 4.6 collective-permute-start.2
  210.1 6.2 %add_add_fusion.2 = f32[32,8,5,768]{3,1,2,0:T(8,128)S(1)} fusion(f32[32,8,5,768]{3,1,2,0:T(8,128)} %fusion.54, f32[768]{0:T(1024)S(1)} %get-tuple-element.182, pred[8,5]{0,1:T(8,128)(4,1)S(1)} %get-tuple-element.185, bf16[3,3,192,768]{3,2,1,0:T(8,128)(2,1)S(1)} %copy-done.3, bf16[34,1,7,2,192]{4,2,3,0,1:T(8,128)(2,1)S(1)} %slice.104, ...), kind=kOutput, calls=%fused_computation.clone.1 | convolution fusion | flops 3403511808 | bytes 11226664 | tf_op jit(solution)/shard_map/while/body/eval_jaxpr/conv_general_dilated | solution.py:10
  222.6 5.4 %collective-permute-start.1 = (bf16[1,1,32,192]{3,1,2,0:T(2,128)(2,1)S(1)}, bf16[1,1,32,192]{3,1,2,0:T(2,128)(2,1)S(1)}, u32[]{:S(2)}, u32[]{:S(2)}) collective-permute-start(bf16[1,1,32,192]{3,1,2,0:T(2,128)(2,1)S(1)} %get-tuple-element.145), channel_id=1, source_target_pairs={{0,1},{1,2},{2,3},{3,4},{4,5},{5,6},{6,7},{8,9},{9,10},{10,11},{11... | collective-permute-start | bytes 36872 | tf_op jit(solution)/shard_map/while/body/eval_jaxpr/ppermute | solution.py:30
  229.2 4.6 collective-permute-start.2
  241.3 6.2 %add_add_fusion.2 = f32[32,8,5,768]{3,1,2,0:T(8,128)S(1)} fusion(f32[32,8,5,768]{3,1,2,0:T(8,128)} %fusion.54, f32[768]{0:T(1024)S(1)} %get-tuple-element.182, pred[8,5]{0,1:T(8,128)(4,1)S(1)} %get-tuple-element.185, bf16[3,3,192,768]{3,2,1,0:T(8,128)(2,1)S(1)} %copy-done.3, bf16[34,1,7,2,192]{4,2,3,0,1:T(8,128)(2,1)S(1)} %slice.104, ...), kind=kOutput, calls=%fused_computation.clone.1 | convolution fusion | flops 3403511808 | bytes 11226664 | tf_op jit(solution)/shard_map/while/body/eval_jaxpr/conv_general_dilated | solution.py:10
  253.7 5.4 %collective-permute-start.1 = (bf16[1,1,32,192]{3,1,2,0:T(2,128)(2,1)S(1)}, bf16[1,1,32,192]{3,1,2,0:T(2,128)(2,1)S(1)}, u32[]{:S(2)}, u32[]{:S(2)}) collective-permute-start(bf16[1,1,32,192]{3,1,2,0:T(2,128)(2,1)S(1)} %get-tuple-element.145), channel_id=1, source_target_pairs={{0,1},{1,2},{2,3},{3,4},{4,5},{5,6},{6,7},{8,9},{9,10},{10,11},{11... | collective-permute-start | bytes 36872 | tf_op jit(solution)/shard_map/while/body/eval_jaxpr/ppermute | solution.py:30
  260.4 4.6 collective-permute-start.2
  272.4 6.2 %add_add_fusion.2 = f32[32,8,5,768]{3,1,2,0:T(8,128)S(1)} fusion(f32[32,8,5,768]{3,1,2,0:T(8,128)} %fusion.54, f32[768]{0:T(1024)S(1)} %get-tuple-element.182, pred[8,5]{0,1:T(8,128)(4,1)S(1)} %get-tuple-element.185, bf16[3,3,192,768]{3,2,1,0:T(8,128)(2,1)S(1)} %copy-done.3, bf16[34,1,7,2,192]{4,2,3,0,1:T(8,128)(2,1)S(1)} %slice.104, ...), kind=kOutput, calls=%fused_computation.clone.1 | convolution fusion | flops 3403511808 | bytes 11226664 | tf_op jit(solution)/shard_map/while/body/eval_jaxpr/conv_general_dilated | solution.py:10
  284.9 5.4 %collective-permute-start.1 = (bf16[1,1,32,192]{3,1,2,0:T(2,128)(2,1)S(1)}, bf16[1,1,32,192]{3,1,2,0:T(2,128)(2,1)S(1)}, u32[]{:S(2)}, u32[]{:S(2)}) collective-permute-start(bf16[1,1,32,192]{3,1,2,0:T(2,128)(2,1)S(1)} %get-tuple-element.145), channel_id=1, source_target_pairs={{0,1},{1,2},{2,3},{3,4},{4,5},{5,6},{6,7},{8,9},{9,10},{10,11},{11... | collective-permute-start | bytes 36872 | tf_op jit(solution)/shard_map/while/body/eval_jaxpr/ppermute | solution.py:30
  291.6 4.6 collective-permute-start.2
  303.6 6.2 %add_add_fusion.2 = f32[32,8,5,768]{3,1,2,0:T(8,128)S(1)} fusion(f32[32,8,5,768]{3,1,2,0:T(8,128)} %fusion.54, f32[768]{0:T(1024)S(1)} %get-tuple-element.182, pred[8,5]{0,1:T(8,128)(4,1)S(1)} %get-tuple-element.185, bf16[3,3,192,768]{3,2,1,0:T(8,128)(2,1)S(1)} %copy-done.3, bf16[34,1,7,2,192]{4,2,3,0,1:T(8,128)(2,1)S(1)} %slice.104, ...), kind=kOutput, calls=%fused_computation.clone.1 | convolution fusion | flops 3403511808 | bytes 11226664 | tf_op jit(solution)/shard_map/while/body/eval_jaxpr/conv_general_dilated | solution.py:10
  316.1 5.4 %collective-permute-start.1 = (bf16[1,1,32,192]{3,1,2,0:T(2,128)(2,1)S(1)}, bf16[1,1,32,192]{3,1,2,0:T(2,128)(2,1)S(1)}, u32[]{:S(2)}, u32[]{:S(2)}) collective-permute-start(bf16[1,1,32,192]{3,1,2,0:T(2,128)(2,1)S(1)} %get-tuple-element.145), channel_id=1, source_target_pairs={{0,1},{1,2},{2,3},{3,4},{4,5},{5,6},{6,7},{8,9},{9,10},{10,11},{11... | collective-permute-start | bytes 36872 | tf_op jit(solution)/shard_map/while/body/eval_jaxpr/ppermute | solution.py:30
  322.8 4.6 collective-permute-start.2
  334.8 6.2 %add_add_fusion.2 = f32[32,8,5,768]{3,1,2,0:T(8,128)S(1)} fusion(f32[32,8,5,768]{3,1,2,0:T(8,128)} %fusion.54, f32[768]{0:T(1024)S(1)} %get-tuple-element.182, pred[8,5]{0,1:T(8,128)(4,1)S(1)} %get-tuple-element.185, bf16[3,3,192,768]{3,2,1,0:T(8,128)(2,1)S(1)} %copy-done.3, bf16[34,1,7,2,192]{4,2,3,0,1:T(8,128)(2,1)S(1)} %slice.104, ...), kind=kOutput, calls=%fused_computation.clone.1 | convolution fusion | flops 3403511808 | bytes 11226664 | tf_op jit(solution)/shard_map/while/body/eval_jaxpr/conv_general_dilated | solution.py:10
  347.3 5.4 %collective-permute-start.1 = (bf16[1,1,32,192]{3,1,2,0:T(2,128)(2,1)S(1)}, bf16[1,1,32,192]{3,1,2,0:T(2,128)(2,1)S(1)}, u32[]{:S(2)}, u32[]{:S(2)}) collective-permute-start(bf16[1,1,32,192]{3,1,2,0:T(2,128)(2,1)S(1)} %get-tuple-element.145), channel_id=1, source_target_pairs={{0,1},{1,2},{2,3},{3,4},{4,5},{5,6},{6,7},{8,9},{9,10},{10,11},{11... | collective-permute-start | bytes 36872 | tf_op jit(solution)/shard_map/while/body/eval_jaxpr/ppermute | solution.py:30
  353.9 4.6 collective-permute-start.2
  366.0 6.2 %add_add_fusion.2 = f32[32,8,5,768]{3,1,2,0:T(8,128)S(1)} fusion(f32[32,8,5,768]{3,1,2,0:T(8,128)} %fusion.54, f32[768]{0:T(1024)S(1)} %get-tuple-element.182, pred[8,5]{0,1:T(8,128)(4,1)S(1)} %get-tuple-element.185, bf16[3,3,192,768]{3,2,1,0:T(8,128)(2,1)S(1)} %copy-done.3, bf16[34,1,7,2,192]{4,2,3,0,1:T(8,128)(2,1)S(1)} %slice.104, ...), kind=kOutput, calls=%fused_computation.clone.1 | convolution fusion | flops 3403511808 | bytes 11226664 | tf_op jit(solution)/shard_map/while/body/eval_jaxpr/conv_general_dilated | solution.py:10
  378.5 5.4 %collective-permute-start.1 = (bf16[1,1,32,192]{3,1,2,0:T(2,128)(2,1)S(1)}, bf16[1,1,32,192]{3,1,2,0:T(2,128)(2,1)S(1)}, u32[]{:S(2)}, u32[]{:S(2)}) collective-permute-start(bf16[1,1,32,192]{3,1,2,0:T(2,128)(2,1)S(1)} %get-tuple-element.145), channel_id=1, source_target_pairs={{0,1},{1,2},{2,3},{3,4},{4,5},{5,6},{6,7},{8,9},{9,10},{10,11},{11... | collective-permute-start | bytes 36872 | tf_op jit(solution)/shard_map/while/body/eval_jaxpr/ppermute | solution.py:30
  385.1 4.6 collective-permute-start.2
  397.2 6.2 %add_add_fusion.2 = f32[32,8,5,768]{3,1,2,0:T(8,128)S(1)} fusion(f32[32,8,5,768]{3,1,2,0:T(8,128)} %fusion.54, f32[768]{0:T(1024)S(1)} %get-tuple-element.182, pred[8,5]{0,1:T(8,128)(4,1)S(1)} %get-tuple-element.185, bf16[3,3,192,768]{3,2,1,0:T(8,128)(2,1)S(1)} %copy-done.3, bf16[34,1,7,2,192]{4,2,3,0,1:T(8,128)(2,1)S(1)} %slice.104, ...), kind=kOutput, calls=%fused_computation.clone.1 | convolution fusion | flops 3403511808 | bytes 11226664 | tf_op jit(solution)/shard_map/while/body/eval_jaxpr/conv_general_dilated | solution.py:10
  409.7 5.4 %collective-permute-start.1 = (bf16[1,1,32,192]{3,1,2,0:T(2,128)(2,1)S(1)}, bf16[1,1,32,192]{3,1,2,0:T(2,128)(2,1)S(1)}, u32[]{:S(2)}, u32[]{:S(2)}) collective-permute-start(bf16[1,1,32,192]{3,1,2,0:T(2,128)(2,1)S(1)} %get-tuple-element.145), channel_id=1, source_target_pairs={{0,1},{1,2},{2,3},{3,4},{4,5},{5,6},{6,7},{8,9},{9,10},{10,11},{11... | collective-permute-start | bytes 36872 | tf_op jit(solution)/shard_map/while/body/eval_jaxpr/ppermute | solution.py:30
  416.3 4.6 collective-permute-start.2
  428.4 6.2 %add_add_fusion.2 = f32[32,8,5,768]{3,1,2,0:T(8,128)S(1)} fusion(f32[32,8,5,768]{3,1,2,0:T(8,128)} %fusion.54, f32[768]{0:T(1024)S(1)} %get-tuple-element.182, pred[8,5]{0,1:T(8,128)(4,1)S(1)} %get-tuple-element.185, bf16[3,3,192,768]{3,2,1,0:T(8,128)(2,1)S(1)} %copy-done.3, bf16[34,1,7,2,192]{4,2,3,0,1:T(8,128)(2,1)S(1)} %slice.104, ...), kind=kOutput, calls=%fused_computation.clone.1 | convolution fusion | flops 3403511808 | bytes 11226664 | tf_op jit(solution)/shard_map/while/body/eval_jaxpr/conv_general_dilated | solution.py:10
  440.8 5.4 %collective-permute-start.1 = (bf16[1,1,32,192]{3,1,2,0:T(2,128)(2,1)S(1)}, bf16[1,1,32,192]{3,1,2,0:T(2,128)(2,1)S(1)}, u32[]{:S(2)}, u32[]{:S(2)}) collective-permute-start(bf16[1,1,32,192]{3,1,2,0:T(2,128)(2,1)S(1)} %get-tuple-element.145), channel_id=1, source_target_pairs={{0,1},{1,2},{2,3},{3,4},{4,5},{5,6},{6,7},{8,9},{9,10},{10,11},{11... | collective-permute-start | bytes 36872 | tf_op jit(solution)/shard_map/while/body/eval_jaxpr/ppermute | solution.py:30
  447.5 4.6 collective-permute-start.2
  459.5 6.2 %add_add_fusion.2 = f32[32,8,5,768]{3,1,2,0:T(8,128)S(1)} fusion(f32[32,8,5,768]{3,1,2,0:T(8,128)} %fusion.54, f32[768]{0:T(1024)S(1)} %get-tuple-element.182, pred[8,5]{0,1:T(8,128)(4,1)S(1)} %get-tuple-element.185, bf16[3,3,192,768]{3,2,1,0:T(8,128)(2,1)S(1)} %copy-done.3, bf16[34,1,7,2,192]{4,2,3,0,1:T(8,128)(2,1)S(1)} %slice.104, ...), kind=kOutput, calls=%fused_computation.clone.1 | convolution fusion | flops 3403511808 | bytes 11226664 | tf_op jit(solution)/shard_map/while/body/eval_jaxpr/conv_general_dilated | solution.py:10
  472.0 5.4 %collective-permute-start.1 = (bf16[1,1,32,192]{3,1,2,0:T(2,128)(2,1)S(1)}, bf16[1,1,32,192]{3,1,2,0:T(2,128)(2,1)S(1)}, u32[]{:S(2)}, u32[]{:S(2)}) collective-permute-start(bf16[1,1,32,192]{3,1,2,0:T(2,128)(2,1)S(1)} %get-tuple-element.145), channel_id=1, source_target_pairs={{0,1},{1,2},{2,3},{3,4},{4,5},{5,6},{6,7},{8,9},{9,10},{10,11},{11... | collective-permute-start | bytes 36872 | tf_op jit(solution)/shard_map/while/body/eval_jaxpr/ppermute | solution.py:30
  478.7 4.6 collective-permute-start.2
  490.7 6.2 %add_add_fusion.2 = f32[32,8,5,768]{3,1,2,0:T(8,128)S(1)} fusion(f32[32,8,5,768]{3,1,2,0:T(8,128)} %fusion.54, f32[768]{0:T(1024)S(1)} %get-tuple-element.182, pred[8,5]{0,1:T(8,128)(4,1)S(1)} %get-tuple-element.185, bf16[3,3,192,768]{3,2,1,0:T(8,128)(2,1)S(1)} %copy-done.3, bf16[34,1,7,2,192]{4,2,3,0,1:T(8,128)(2,1)S(1)} %slice.104, ...), kind=kOutput, calls=%fused_computation.clone.1 | convolution fusion | flops 3403511808 | bytes 11226664 | tf_op jit(solution)/shard_map/while/body/eval_jaxpr/conv_general_dilated | solution.py:10
  503.2 5.4 %collective-permute-start.1 = (bf16[1,1,32,192]{3,1,2,0:T(2,128)(2,1)S(1)}, bf16[1,1,32,192]{3,1,2,0:T(2,128)(2,1)S(1)}, u32[]{:S(2)}, u32[]{:S(2)}) collective-permute-start(bf16[1,1,32,192]{3,1,2,0:T(2,128)(2,1)S(1)} %get-tuple-element.145), channel_id=1, source_target_pairs={{0,1},{1,2},{2,3},{3,4},{4,5},{5,6},{6,7},{8,9},{9,10},{10,11},{11... | collective-permute-start | bytes 36872 | tf_op jit(solution)/shard_map/while/body/eval_jaxpr/ppermute | solution.py:30
  509.9 4.6 collective-permute-start.2
  521.9 6.2 %add_add_fusion.2 = f32[32,8,5,768]{3,1,2,0:T(8,128)S(1)} fusion(f32[32,8,5,768]{3,1,2,0:T(8,128)} %fusion.54, f32[768]{0:T(1024)S(1)} %get-tuple-element.182, pred[8,5]{0,1:T(8,128)(4,1)S(1)} %get-tuple-element.185, bf16[3,3,192,768]{3,2,1,0:T(8,128)(2,1)S(1)} %copy-done.3, bf16[34,1,7,2,192]{4,2,3,0,1:T(8,128)(2,1)S(1)} %slice.104, ...), kind=kOutput, calls=%fused_computation.clone.1 | convolution fusion | flops 3403511808 | bytes 11226664 | tf_op jit(solution)/shard_map/while/body/eval_jaxpr/conv_general_dilated | solution.py:10
  (429 shorter events, 272.6 us)
Async XLA Ops:
  5.2 7.1 %collective-permute-start.4 = (bf16[16,1,1,32,64]{4,2,3,1,0:T(2,128)(2,1)S(1)}, bf16[16,1,1,32,64]{4,2,3,1,0:T(2,128)(2,1)S(1)}, u32[]{:S(2)}, u32[]{:S(2)}) collective-permute-start(bf16[16,1,1,32,64]{4,2,3,1,0:T(2,128)(2,1)S(1)} %get-tuple-element.84), channel_id=1, source_target_pairs={{0,1},{1,2},{2,3},{3,4},{4,5},{5,6},{6,7},{8,9},{9,10},{10,11},{11... | collective-permute-start | bytes 196616 | tf_op jit(solution)/shard_map/ppermute | solution.py:30
  9.0 7.8 %collective-permute-start.5 = (bf16[16,1,1,32,64]{4,2,3,1,0:T(2,128)(2,1)S(1)}, bf16[16,1,1,32,64]{4,2,3,1,0:T(2,128)(2,1)S(1)}, u32[]{:S(2)}, u32[]{:S(2)}) collective-permute-start(bf16[16,1,1,32,64]{4,2,3,1,0:T(2,128)(2,1)S(1)} %get-tuple-element.85), channel_id=1, source_target_pairs={{1,0},{2,1},{3,2},{4,3},{5,4},{6,5},{7,6},{9,8},{10,9},{11,10},{12... | collective-permute-start | bytes 196616 | tf_op jit(solution)/shard_map/ppermute | solution.py:31
  17.0 8.4 %collective-permute-start.6 = (bf16[16,1,34,1,64]{4,2,3,1,0:T(8,128)(2,1)S(1)}, bf16[16,1,34,1,64]{4,2,3,1,0:T(8,128)(2,1)}, u32[]{:S(2)}, u32[]{:S(2)}) collective-permute-start(bf16[16,1,34,1,64]{4,2,3,1,0:T(8,128)(2,1)S(1)} %get-tuple-element.82), channel_id=1, source_target_pairs={{0,8},{8,16},{16,24},{24,32},{32,40},{40,48},{48,56},{56,64},{64,7... | collective-permute-start | bytes 208904 | tf_op jit(solution)/shard_map/ppermute | solution.py:30
  33.3 7.2 %collective-permute-start = (bf16[1,1,32,192]{3,1,2,0:T(2,128)(2,1)S(1)}, bf16[1,1,32,192]{3,1,2,0:T(2,128)(2,1)S(1)}, u32[]{:S(2)}, u32[]{:S(2)}) collective-permute-start(bf16[1,1,32,192]{3,1,2,0:T(2,128)(2,1)S(1)} %get-tuple-element.144), channel_id=1, source_target_pairs={{1,0},{2,1},{3,2},{4,3},{5,4},{6,5},{7,6},{9,8},{10,9},{11,10},{12... | collective-permute-start | bytes 36872 | tf_op jit(solution)/shard_map/while/body/eval_jaxpr/ppermute | solution.py:31
  40.5 11.9 %collective-permute-start.2 = (bf16[1,34,1,192]{3,1,2,0:T(8,128)(2,1)S(1)}, bf16[1,34,1,192]{3,1,2,0:T(8,128)(2,1)S(1)}, u32[]{:S(2)}, u32[]{:S(2)}) collective-permute-start(bf16[1,34,1,192]{3,1,2,0:T(8,128)(2,1)S(1)} %get-tuple-element.146), channel_id=1, source_target_pairs={{8,0},{16,8},{24,16},{32,24},{40,32},{48,40},{56,48},{64,56},{72,6... | collective-permute-start | bytes 39176 | tf_op jit(solution)/shard_map/while/body/eval_jaxpr/ppermute | solution.py:31
  46.8 6.6 %collective-permute-start.3 = (bf16[1,34,1,192]{3,1,2,0:T(8,128)(2,1)S(1)}, bf16[1,34,1,192]{3,1,2,0:T(8,128)(2,1)S(1)}, u32[]{:S(2)}, u32[]{:S(2)}) collective-permute-start(bf16[1,34,1,192]{3,1,2,0:T(8,128)(2,1)S(1)} %get-tuple-element.147), channel_id=1, source_target_pairs={{0,8},{8,16},{16,24},{24,32},{32,40},{40,48},{48,56},{56,64},{64,7... | collective-permute-start | bytes 39176 | tf_op jit(solution)/shard_map/while/body/eval_jaxpr/ppermute | solution.py:30
  64.7 8.5 %collective-permute-start = (bf16[1,1,32,192]{3,1,2,0:T(2,128)(2,1)S(1)}, bf16[1,1,32,192]{3,1,2,0:T(2,128)(2,1)S(1)}, u32[]{:S(2)}, u32[]{:S(2)}) collective-permute-start(bf16[1,1,32,192]{3,1,2,0:T(2,128)(2,1)S(1)} %get-tuple-element.144), channel_id=1, source_target_pairs={{1,0},{2,1},{3,2},{4,3},{5,4},{6,5},{7,6},{9,8},{10,9},{11,10},{12... | collective-permute-start | bytes 36872 | tf_op jit(solution)/shard_map/while/body/eval_jaxpr/ppermute | solution.py:31
  73.3 10.3 %collective-permute-start.2 = (bf16[1,34,1,192]{3,1,2,0:T(8,128)(2,1)S(1)}, bf16[1,34,1,192]{3,1,2,0:T(8,128)(2,1)S(1)}, u32[]{:S(2)}, u32[]{:S(2)}) collective-permute-start(bf16[1,34,1,192]{3,1,2,0:T(8,128)(2,1)S(1)} %get-tuple-element.146), channel_id=1, source_target_pairs={{8,0},{16,8},{24,16},{32,24},{40,32},{48,40},{56,48},{64,56},{72,6... | collective-permute-start | bytes 39176 | tf_op jit(solution)/shard_map/while/body/eval_jaxpr/ppermute | solution.py:31
  77.9 6.6 %collective-permute-start.3 = (bf16[1,34,1,192]{3,1,2,0:T(8,128)(2,1)S(1)}, bf16[1,34,1,192]{3,1,2,0:T(8,128)(2,1)S(1)}, u32[]{:S(2)}, u32[]{:S(2)}) collective-permute-start(bf16[1,34,1,192]{3,1,2,0:T(8,128)(2,1)S(1)} %get-tuple-element.147), channel_id=1, source_target_pairs={{0,8},{8,16},{16,24},{24,32},{32,40},{40,48},{48,56},{56,64},{64,7... | collective-permute-start | bytes 39176 | tf_op jit(solution)/shard_map/while/body/eval_jaxpr/ppermute | solution.py:30
  95.9 8.5 %collective-permute-start = (bf16[1,1,32,192]{3,1,2,0:T(2,128)(2,1)S(1)}, bf16[1,1,32,192]{3,1,2,0:T(2,128)(2,1)S(1)}, u32[]{:S(2)}, u32[]{:S(2)}) collective-permute-start(bf16[1,1,32,192]{3,1,2,0:T(2,128)(2,1)S(1)} %get-tuple-element.144), channel_id=1, source_target_pairs={{1,0},{2,1},{3,2},{4,3},{5,4},{6,5},{7,6},{9,8},{10,9},{11,10},{12... | collective-permute-start | bytes 36872 | tf_op jit(solution)/shard_map/while/body/eval_jaxpr/ppermute | solution.py:31
  104.5 10.3 %collective-permute-start.2 = (bf16[1,34,1,192]{3,1,2,0:T(8,128)(2,1)S(1)}, bf16[1,34,1,192]{3,1,2,0:T(8,128)(2,1)S(1)}, u32[]{:S(2)}, u32[]{:S(2)}) collective-permute-start(bf16[1,34,1,192]{3,1,2,0:T(8,128)(2,1)S(1)} %get-tuple-element.146), channel_id=1, source_target_pairs={{8,0},{16,8},{24,16},{32,24},{40,32},{48,40},{56,48},{64,56},{72,6... | collective-permute-start | bytes 39176 | tf_op jit(solution)/shard_map/while/body/eval_jaxpr/ppermute | solution.py:31
  109.1 6.6 %collective-permute-start.3 = (bf16[1,34,1,192]{3,1,2,0:T(8,128)(2,1)S(1)}, bf16[1,34,1,192]{3,1,2,0:T(8,128)(2,1)S(1)}, u32[]{:S(2)}, u32[]{:S(2)}) collective-permute-start(bf16[1,34,1,192]{3,1,2,0:T(8,128)(2,1)S(1)} %get-tuple-element.147), channel_id=1, source_target_pairs={{0,8},{8,16},{16,24},{24,32},{32,40},{40,48},{48,56},{56,64},{64,7... | collective-permute-start | bytes 39176 | tf_op jit(solution)/shard_map/while/body/eval_jaxpr/ppermute | solution.py:30
  127.1 8.5 %collective-permute-start = (bf16[1,1,32,192]{3,1,2,0:T(2,128)(2,1)S(1)}, bf16[1,1,32,192]{3,1,2,0:T(2,128)(2,1)S(1)}, u32[]{:S(2)}, u32[]{:S(2)}) collective-permute-start(bf16[1,1,32,192]{3,1,2,0:T(2,128)(2,1)S(1)} %get-tuple-element.144), channel_id=1, source_target_pairs={{1,0},{2,1},{3,2},{4,3},{5,4},{6,5},{7,6},{9,8},{10,9},{11,10},{12... | collective-permute-start | bytes 36872 | tf_op jit(solution)/shard_map/while/body/eval_jaxpr/ppermute | solution.py:31
  135.7 10.3 %collective-permute-start.2 = (bf16[1,34,1,192]{3,1,2,0:T(8,128)(2,1)S(1)}, bf16[1,34,1,192]{3,1,2,0:T(8,128)(2,1)S(1)}, u32[]{:S(2)}, u32[]{:S(2)}) collective-permute-start(bf16[1,34,1,192]{3,1,2,0:T(8,128)(2,1)S(1)} %get-tuple-element.146), channel_id=1, source_target_pairs={{8,0},{16,8},{24,16},{32,24},{40,32},{48,40},{56,48},{64,56},{72,6... | collective-permute-start | bytes 39176 | tf_op jit(solution)/shard_map/while/body/eval_jaxpr/ppermute | solution.py:31
  140.3 6.6 %collective-permute-start.3 = (bf16[1,34,1,192]{3,1,2,0:T(8,128)(2,1)S(1)}, bf16[1,34,1,192]{3,1,2,0:T(8,128)(2,1)S(1)}, u32[]{:S(2)}, u32[]{:S(2)}) collective-permute-start(bf16[1,34,1,192]{3,1,2,0:T(8,128)(2,1)S(1)} %get-tuple-element.147), channel_id=1, source_target_pairs={{0,8},{8,16},{16,24},{24,32},{32,40},{40,48},{48,56},{56,64},{64,7... | collective-permute-start | bytes 39176 | tf_op jit(solution)/shard_map/while/body/eval_jaxpr/ppermute | solution.py:30
  158.3 8.5 %collective-permute-start = (bf16[1,1,32,192]{3,1,2,0:T(2,128)(2,1)S(1)}, bf16[1,1,32,192]{3,1,2,0:T(2,128)(2,1)S(1)}, u32[]{:S(2)}, u32[]{:S(2)}) collective-permute-start(bf16[1,1,32,192]{3,1,2,0:T(2,128)(2,1)S(1)} %get-tuple-element.144), channel_id=1, source_target_pairs={{1,0},{2,1},{3,2},{4,3},{5,4},{6,5},{7,6},{9,8},{10,9},{11,10},{12... | collective-permute-start | bytes 36872 | tf_op jit(solution)/shard_map/while/body/eval_jaxpr/ppermute | solution.py:31
  166.8 10.3 %collective-permute-start.2 = (bf16[1,34,1,192]{3,1,2,0:T(8,128)(2,1)S(1)}, bf16[1,34,1,192]{3,1,2,0:T(8,128)(2,1)S(1)}, u32[]{:S(2)}, u32[]{:S(2)}) collective-permute-start(bf16[1,34,1,192]{3,1,2,0:T(8,128)(2,1)S(1)} %get-tuple-element.146), channel_id=1, source_target_pairs={{8,0},{16,8},{24,16},{32,24},{40,32},{48,40},{56,48},{64,56},{72,6... | collective-permute-start | bytes 39176 | tf_op jit(solution)/shard_map/while/body/eval_jaxpr/ppermute | solution.py:31
  171.5 6.6 %collective-permute-start.3 = (bf16[1,34,1,192]{3,1,2,0:T(8,128)(2,1)S(1)}, bf16[1,34,1,192]{3,1,2,0:T(8,128)(2,1)S(1)}, u32[]{:S(2)}, u32[]{:S(2)}) collective-permute-start(bf16[1,34,1,192]{3,1,2,0:T(8,128)(2,1)S(1)} %get-tuple-element.147), channel_id=1, source_target_pairs={{0,8},{8,16},{16,24},{24,32},{32,40},{40,48},{48,56},{56,64},{64,7... | collective-permute-start | bytes 39176 | tf_op jit(solution)/shard_map/while/body/eval_jaxpr/ppermute | solution.py:30
  189.5 8.5 %collective-permute-start = (bf16[1,1,32,192]{3,1,2,0:T(2,128)(2,1)S(1)}, bf16[1,1,32,192]{3,1,2,0:T(2,128)(2,1)S(1)}, u32[]{:S(2)}, u32[]{:S(2)}) collective-permute-start(bf16[1,1,32,192]{3,1,2,0:T(2,128)(2,1)S(1)} %get-tuple-element.144), channel_id=1, source_target_pairs={{1,0},{2,1},{3,2},{4,3},{5,4},{6,5},{7,6},{9,8},{10,9},{11,10},{12... | collective-permute-start | bytes 36872 | tf_op jit(solution)/shard_map/while/body/eval_jaxpr/ppermute | solution.py:31
  198.0 10.3 %collective-permute-start.2 = (bf16[1,34,1,192]{3,1,2,0:T(8,128)(2,1)S(1)}, bf16[1,34,1,192]{3,1,2,0:T(8,128)(2,1)S(1)}, u32[]{:S(2)}, u32[]{:S(2)}) collective-permute-start(bf16[1,34,1,192]{3,1,2,0:T(8,128)(2,1)S(1)} %get-tuple-element.146), channel_id=1, source_target_pairs={{8,0},{16,8},{24,16},{32,24},{40,32},{48,40},{56,48},{64,56},{72,6... | collective-permute-start | bytes 39176 | tf_op jit(solution)/shard_map/while/body/eval_jaxpr/ppermute | solution.py:31
  202.7 6.6 %collective-permute-start.3 = (bf16[1,34,1,192]{3,1,2,0:T(8,128)(2,1)S(1)}, bf16[1,34,1,192]{3,1,2,0:T(8,128)(2,1)S(1)}, u32[]{:S(2)}, u32[]{:S(2)}) collective-permute-start(bf16[1,34,1,192]{3,1,2,0:T(8,128)(2,1)S(1)} %get-tuple-element.147), channel_id=1, source_target_pairs={{0,8},{8,16},{16,24},{24,32},{32,40},{40,48},{48,56},{56,64},{64,7... | collective-permute-start | bytes 39176 | tf_op jit(solution)/shard_map/while/body/eval_jaxpr/ppermute | solution.py:30
  220.6 8.5 %collective-permute-start = (bf16[1,1,32,192]{3,1,2,0:T(2,128)(2,1)S(1)}, bf16[1,1,32,192]{3,1,2,0:T(2,128)(2,1)S(1)}, u32[]{:S(2)}, u32[]{:S(2)}) collective-permute-start(bf16[1,1,32,192]{3,1,2,0:T(2,128)(2,1)S(1)} %get-tuple-element.144), channel_id=1, source_target_pairs={{1,0},{2,1},{3,2},{4,3},{5,4},{6,5},{7,6},{9,8},{10,9},{11,10},{12... | collective-permute-start | bytes 36872 | tf_op jit(solution)/shard_map/while/body/eval_jaxpr/ppermute | solution.py:31
  229.2 10.3 %collective-permute-start.2 = (bf16[1,34,1,192]{3,1,2,0:T(8,128)(2,1)S(1)}, bf16[1,34,1,192]{3,1,2,0:T(8,128)(2,1)S(1)}, u32[]{:S(2)}, u32[]{:S(2)}) collective-permute-start(bf16[1,34,1,192]{3,1,2,0:T(8,128)(2,1)S(1)} %get-tuple-element.146), channel_id=1, source_target_pairs={{8,0},{16,8},{24,16},{32,24},{40,32},{48,40},{56,48},{64,56},{72,6... | collective-permute-start | bytes 39176 | tf_op jit(solution)/shard_map/while/body/eval_jaxpr/ppermute | solution.py:31
  233.9 6.6 %collective-permute-start.3 = (bf16[1,34,1,192]{3,1,2,0:T(8,128)(2,1)S(1)}, bf16[1,34,1,192]{3,1,2,0:T(8,128)(2,1)S(1)}, u32[]{:S(2)}, u32[]{:S(2)}) collective-permute-start(bf16[1,34,1,192]{3,1,2,0:T(8,128)(2,1)S(1)} %get-tuple-element.147), channel_id=1, source_target_pairs={{0,8},{8,16},{16,24},{24,32},{32,40},{40,48},{48,56},{56,64},{64,7... | collective-permute-start | bytes 39176 | tf_op jit(solution)/shard_map/while/body/eval_jaxpr/ppermute | solution.py:30
  251.8 8.5 %collective-permute-start = (bf16[1,1,32,192]{3,1,2,0:T(2,128)(2,1)S(1)}, bf16[1,1,32,192]{3,1,2,0:T(2,128)(2,1)S(1)}, u32[]{:S(2)}, u32[]{:S(2)}) collective-permute-start(bf16[1,1,32,192]{3,1,2,0:T(2,128)(2,1)S(1)} %get-tuple-element.144), channel_id=1, source_target_pairs={{1,0},{2,1},{3,2},{4,3},{5,4},{6,5},{7,6},{9,8},{10,9},{11,10},{12... | collective-permute-start | bytes 36872 | tf_op jit(solution)/shard_map/while/body/eval_jaxpr/ppermute | solution.py:31
  260.4 10.3 %collective-permute-start.2 = (bf16[1,34,1,192]{3,1,2,0:T(8,128)(2,1)S(1)}, bf16[1,34,1,192]{3,1,2,0:T(8,128)(2,1)S(1)}, u32[]{:S(2)}, u32[]{:S(2)}) collective-permute-start(bf16[1,34,1,192]{3,1,2,0:T(8,128)(2,1)S(1)} %get-tuple-element.146), channel_id=1, source_target_pairs={{8,0},{16,8},{24,16},{32,24},{40,32},{48,40},{56,48},{64,56},{72,6... | collective-permute-start | bytes 39176 | tf_op jit(solution)/shard_map/while/body/eval_jaxpr/ppermute | solution.py:31
  265.0 6.6 %collective-permute-start.3 = (bf16[1,34,1,192]{3,1,2,0:T(8,128)(2,1)S(1)}, bf16[1,34,1,192]{3,1,2,0:T(8,128)(2,1)S(1)}, u32[]{:S(2)}, u32[]{:S(2)}) collective-permute-start(bf16[1,34,1,192]{3,1,2,0:T(8,128)(2,1)S(1)} %get-tuple-element.147), channel_id=1, source_target_pairs={{0,8},{8,16},{16,24},{24,32},{32,40},{40,48},{48,56},{56,64},{64,7... | collective-permute-start | bytes 39176 | tf_op jit(solution)/shard_map/while/body/eval_jaxpr/ppermute | solution.py:30
  283.0 8.5 %collective-permute-start = (bf16[1,1,32,192]{3,1,2,0:T(2,128)(2,1)S(1)}, bf16[1,1,32,192]{3,1,2,0:T(2,128)(2,1)S(1)}, u32[]{:S(2)}, u32[]{:S(2)}) collective-permute-start(bf16[1,1,32,192]{3,1,2,0:T(2,128)(2,1)S(1)} %get-tuple-element.144), channel_id=1, source_target_pairs={{1,0},{2,1},{3,2},{4,3},{5,4},{6,5},{7,6},{9,8},{10,9},{11,10},{12... | collective-permute-start | bytes 36872 | tf_op jit(solution)/shard_map/while/body/eval_jaxpr/ppermute | solution.py:31
  291.6 10.3 %collective-permute-start.2 = (bf16[1,34,1,192]{3,1,2,0:T(8,128)(2,1)S(1)}, bf16[1,34,1,192]{3,1,2,0:T(8,128)(2,1)S(1)}, u32[]{:S(2)}, u32[]{:S(2)}) collective-permute-start(bf16[1,34,1,192]{3,1,2,0:T(8,128)(2,1)S(1)} %get-tuple-element.146), channel_id=1, source_target_pairs={{8,0},{16,8},{24,16},{32,24},{40,32},{48,40},{56,48},{64,56},{72,6... | collective-permute-start | bytes 39176 | tf_op jit(solution)/shard_map/while/body/eval_jaxpr/ppermute | solution.py:31
  314.2 8.5 %collective-permute-start = (bf16[1,1,32,192]{3,1,2,0:T(2,128)(2,1)S(1)}, bf16[1,1,32,192]{3,1,2,0:T(2,128)(2,1)S(1)}, u32[]{:S(2)}, u32[]{:S(2)}) collective-permute-start(bf16[1,1,32,192]{3,1,2,0:T(2,128)(2,1)S(1)} %get-tuple-element.144), channel_id=1, source_target_pairs={{1,0},{2,1},{3,2},{4,3},{5,4},{6,5},{7,6},{9,8},{10,9},{11,10},{12... | collective-permute-start | bytes 36872 | tf_op jit(solution)/shard_map/while/body/eval_jaxpr/ppermute | solution.py:31
  322.8 10.3 %collective-permute-start.2 = (bf16[1,34,1,192]{3,1,2,0:T(8,128)(2,1)S(1)}, bf16[1,34,1,192]{3,1,2,0:T(8,128)(2,1)S(1)}, u32[]{:S(2)}, u32[]{:S(2)}) collective-permute-start(bf16[1,34,1,192]{3,1,2,0:T(8,128)(2,1)S(1)} %get-tuple-element.146), channel_id=1, source_target_pairs={{8,0},{16,8},{24,16},{32,24},{40,32},{48,40},{56,48},{64,56},{72,6... | collective-permute-start | bytes 39176 | tf_op jit(solution)/shard_map/while/body/eval_jaxpr/ppermute | solution.py:31
  345.4 8.5 %collective-permute-start = (bf16[1,1,32,192]{3,1,2,0:T(2,128)(2,1)S(1)}, bf16[1,1,32,192]{3,1,2,0:T(2,128)(2,1)S(1)}, u32[]{:S(2)}, u32[]{:S(2)}) collective-permute-start(bf16[1,1,32,192]{3,1,2,0:T(2,128)(2,1)S(1)} %get-tuple-element.144), channel_id=1, source_target_pairs={{1,0},{2,1},{3,2},{4,3},{5,4},{6,5},{7,6},{9,8},{10,9},{11,10},{12... | collective-permute-start | bytes 36872 | tf_op jit(solution)/shard_map/while/body/eval_jaxpr/ppermute | solution.py:31
  353.9 10.3 %collective-permute-start.2 = (bf16[1,34,1,192]{3,1,2,0:T(8,128)(2,1)S(1)}, bf16[1,34,1,192]{3,1,2,0:T(8,128)(2,1)S(1)}, u32[]{:S(2)}, u32[]{:S(2)}) collective-permute-start(bf16[1,34,1,192]{3,1,2,0:T(8,128)(2,1)S(1)} %get-tuple-element.146), channel_id=1, source_target_pairs={{8,0},{16,8},{24,16},{32,24},{40,32},{48,40},{56,48},{64,56},{72,6... | collective-permute-start | bytes 39176 | tf_op jit(solution)/shard_map/while/body/eval_jaxpr/ppermute | solution.py:31
  358.6 6.6 %collective-permute-start.3 = (bf16[1,34,1,192]{3,1,2,0:T(8,128)(2,1)S(1)}, bf16[1,34,1,192]{3,1,2,0:T(8,128)(2,1)S(1)}, u32[]{:S(2)}, u32[]{:S(2)}) collective-permute-start(bf16[1,34,1,192]{3,1,2,0:T(8,128)(2,1)S(1)} %get-tuple-element.147), channel_id=1, source_target_pairs={{0,8},{8,16},{16,24},{24,32},{32,40},{40,48},{48,56},{56,64},{64,7... | collective-permute-start | bytes 39176 | tf_op jit(solution)/shard_map/while/body/eval_jaxpr/ppermute | solution.py:30
  376.6 8.5 %collective-permute-start = (bf16[1,1,32,192]{3,1,2,0:T(2,128)(2,1)S(1)}, bf16[1,1,32,192]{3,1,2,0:T(2,128)(2,1)S(1)}, u32[]{:S(2)}, u32[]{:S(2)}) collective-permute-start(bf16[1,1,32,192]{3,1,2,0:T(2,128)(2,1)S(1)} %get-tuple-element.144), channel_id=1, source_target_pairs={{1,0},{2,1},{3,2},{4,3},{5,4},{6,5},{7,6},{9,8},{10,9},{11,10},{12... | collective-permute-start | bytes 36872 | tf_op jit(solution)/shard_map/while/body/eval_jaxpr/ppermute | solution.py:31
  385.1 10.3 %collective-permute-start.2 = (bf16[1,34,1,192]{3,1,2,0:T(8,128)(2,1)S(1)}, bf16[1,34,1,192]{3,1,2,0:T(8,128)(2,1)S(1)}, u32[]{:S(2)}, u32[]{:S(2)}) collective-permute-start(bf16[1,34,1,192]{3,1,2,0:T(8,128)(2,1)S(1)} %get-tuple-element.146), channel_id=1, source_target_pairs={{8,0},{16,8},{24,16},{32,24},{40,32},{48,40},{56,48},{64,56},{72,6... | collective-permute-start | bytes 39176 | tf_op jit(solution)/shard_map/while/body/eval_jaxpr/ppermute | solution.py:31
  389.8 6.6 %collective-permute-start.3 = (bf16[1,34,1,192]{3,1,2,0:T(8,128)(2,1)S(1)}, bf16[1,34,1,192]{3,1,2,0:T(8,128)(2,1)S(1)}, u32[]{:S(2)}, u32[]{:S(2)}) collective-permute-start(bf16[1,34,1,192]{3,1,2,0:T(8,128)(2,1)S(1)} %get-tuple-element.147), channel_id=1, source_target_pairs={{0,8},{8,16},{16,24},{24,32},{32,40},{40,48},{48,56},{56,64},{64,7... | collective-permute-start | bytes 39176 | tf_op jit(solution)/shard_map/while/body/eval_jaxpr/ppermute | solution.py:30
  407.7 8.5 %collective-permute-start = (bf16[1,1,32,192]{3,1,2,0:T(2,128)(2,1)S(1)}, bf16[1,1,32,192]{3,1,2,0:T(2,128)(2,1)S(1)}, u32[]{:S(2)}, u32[]{:S(2)}) collective-permute-start(bf16[1,1,32,192]{3,1,2,0:T(2,128)(2,1)S(1)} %get-tuple-element.144), channel_id=1, source_target_pairs={{1,0},{2,1},{3,2},{4,3},{5,4},{6,5},{7,6},{9,8},{10,9},{11,10},{12... | collective-permute-start | bytes 36872 | tf_op jit(solution)/shard_map/while/body/eval_jaxpr/ppermute | solution.py:31
  416.3 10.3 %collective-permute-start.2 = (bf16[1,34,1,192]{3,1,2,0:T(8,128)(2,1)S(1)}, bf16[1,34,1,192]{3,1,2,0:T(8,128)(2,1)S(1)}, u32[]{:S(2)}, u32[]{:S(2)}) collective-permute-start(bf16[1,34,1,192]{3,1,2,0:T(8,128)(2,1)S(1)} %get-tuple-element.146), channel_id=1, source_target_pairs={{8,0},{16,8},{24,16},{32,24},{40,32},{48,40},{56,48},{64,56},{72,6... | collective-permute-start | bytes 39176 | tf_op jit(solution)/shard_map/while/body/eval_jaxpr/ppermute | solution.py:31
  421.0 6.6 %collective-permute-start.3 = (bf16[1,34,1,192]{3,1,2,0:T(8,128)(2,1)S(1)}, bf16[1,34,1,192]{3,1,2,0:T(8,128)(2,1)S(1)}, u32[]{:S(2)}, u32[]{:S(2)}) collective-permute-start(bf16[1,34,1,192]{3,1,2,0:T(8,128)(2,1)S(1)} %get-tuple-element.147), channel_id=1, source_target_pairs={{0,8},{8,16},{16,24},{24,32},{32,40},{40,48},{48,56},{56,64},{64,7... | collective-permute-start | bytes 39176 | tf_op jit(solution)/shard_map/while/body/eval_jaxpr/ppermute | solution.py:30
  438.9 8.5 %collective-permute-start = (bf16[1,1,32,192]{3,1,2,0:T(2,128)(2,1)S(1)}, bf16[1,1,32,192]{3,1,2,0:T(2,128)(2,1)S(1)}, u32[]{:S(2)}, u32[]{:S(2)}) collective-permute-start(bf16[1,1,32,192]{3,1,2,0:T(2,128)(2,1)S(1)} %get-tuple-element.144), channel_id=1, source_target_pairs={{1,0},{2,1},{3,2},{4,3},{5,4},{6,5},{7,6},{9,8},{10,9},{11,10},{12... | collective-permute-start | bytes 36872 | tf_op jit(solution)/shard_map/while/body/eval_jaxpr/ppermute | solution.py:31
  447.5 10.3 %collective-permute-start.2 = (bf16[1,34,1,192]{3,1,2,0:T(8,128)(2,1)S(1)}, bf16[1,34,1,192]{3,1,2,0:T(8,128)(2,1)S(1)}, u32[]{:S(2)}, u32[]{:S(2)}) collective-permute-start(bf16[1,34,1,192]{3,1,2,0:T(8,128)(2,1)S(1)} %get-tuple-element.146), channel_id=1, source_target_pairs={{8,0},{16,8},{24,16},{32,24},{40,32},{48,40},{56,48},{64,56},{72,6... | collective-permute-start | bytes 39176 | tf_op jit(solution)/shard_map/while/body/eval_jaxpr/ppermute | solution.py:31
  452.1 6.6 %collective-permute-start.3 = (bf16[1,34,1,192]{3,1,2,0:T(8,128)(2,1)S(1)}, bf16[1,34,1,192]{3,1,2,0:T(8,128)(2,1)S(1)}, u32[]{:S(2)}, u32[]{:S(2)}) collective-permute-start(bf16[1,34,1,192]{3,1,2,0:T(8,128)(2,1)S(1)} %get-tuple-element.147), channel_id=1, source_target_pairs={{0,8},{8,16},{16,24},{24,32},{32,40},{40,48},{48,56},{56,64},{64,7... | collective-permute-start | bytes 39176 | tf_op jit(solution)/shard_map/while/body/eval_jaxpr/ppermute | solution.py:30
  470.1 8.5 %collective-permute-start = (bf16[1,1,32,192]{3,1,2,0:T(2,128)(2,1)S(1)}, bf16[1,1,32,192]{3,1,2,0:T(2,128)(2,1)S(1)}, u32[]{:S(2)}, u32[]{:S(2)}) collective-permute-start(bf16[1,1,32,192]{3,1,2,0:T(2,128)(2,1)S(1)} %get-tuple-element.144), channel_id=1, source_target_pairs={{1,0},{2,1},{3,2},{4,3},{5,4},{6,5},{7,6},{9,8},{10,9},{11,10},{12... | collective-permute-start | bytes 36872 | tf_op jit(solution)/shard_map/while/body/eval_jaxpr/ppermute | solution.py:31
  478.7 10.3 %collective-permute-start.2 = (bf16[1,34,1,192]{3,1,2,0:T(8,128)(2,1)S(1)}, bf16[1,34,1,192]{3,1,2,0:T(8,128)(2,1)S(1)}, u32[]{:S(2)}, u32[]{:S(2)}) collective-permute-start(bf16[1,34,1,192]{3,1,2,0:T(8,128)(2,1)S(1)} %get-tuple-element.146), channel_id=1, source_target_pairs={{8,0},{16,8},{24,16},{32,24},{40,32},{48,40},{56,48},{64,56},{72,6... | collective-permute-start | bytes 39176 | tf_op jit(solution)/shard_map/while/body/eval_jaxpr/ppermute | solution.py:31
  483.3 6.6 %collective-permute-start.3 = (bf16[1,34,1,192]{3,1,2,0:T(8,128)(2,1)S(1)}, bf16[1,34,1,192]{3,1,2,0:T(8,128)(2,1)S(1)}, u32[]{:S(2)}, u32[]{:S(2)}) collective-permute-start(bf16[1,34,1,192]{3,1,2,0:T(8,128)(2,1)S(1)} %get-tuple-element.147), channel_id=1, source_target_pairs={{0,8},{8,16},{16,24},{24,32},{32,40},{40,48},{48,56},{56,64},{64,7... | collective-permute-start | bytes 39176 | tf_op jit(solution)/shard_map/while/body/eval_jaxpr/ppermute | solution.py:30
  501.3 8.5 %collective-permute-start = (bf16[1,1,32,192]{3,1,2,0:T(2,128)(2,1)S(1)}, bf16[1,1,32,192]{3,1,2,0:T(2,128)(2,1)S(1)}, u32[]{:S(2)}, u32[]{:S(2)}) collective-permute-start(bf16[1,1,32,192]{3,1,2,0:T(2,128)(2,1)S(1)} %get-tuple-element.144), channel_id=1, source_target_pairs={{1,0},{2,1},{3,2},{4,3},{5,4},{6,5},{7,6},{9,8},{10,9},{11,10},{12... | collective-permute-start | bytes 36872 | tf_op jit(solution)/shard_map/while/body/eval_jaxpr/ppermute | solution.py:31
  509.9 10.3 %collective-permute-start.2 = (bf16[1,34,1,192]{3,1,2,0:T(8,128)(2,1)S(1)}, bf16[1,34,1,192]{3,1,2,0:T(8,128)(2,1)S(1)}, u32[]{:S(2)}, u32[]{:S(2)}) collective-permute-start(bf16[1,34,1,192]{3,1,2,0:T(8,128)(2,1)S(1)} %get-tuple-element.146), channel_id=1, source_target_pairs={{8,0},{16,8},{24,16},{32,24},{40,32},{48,40},{56,48},{64,56},{72,6... | collective-permute-start | bytes 39176 | tf_op jit(solution)/shard_map/while/body/eval_jaxpr/ppermute | solution.py:31
  (42 other events, 229.5 us)
where the time goes:
time: 541 us; the launch traced here: 534 us
  starting transfers between devices  235 us (43%)
  matrix products  159 us (29%)
  local copies, waits for them, and re-layouts  70.9 us (13%)
  other arithmetic  42.5 us (8%)
  waiting for transfers between devices  22.8 us (4%)
    conv_general_dilated x32, matrix products, conv_valid(): lax.conv_general_dilated(operand, kernel, (1, 1), 'VALID', dimension_numb...  159 us
    ppermute x34, starting transfers between devices, edge_exchange(): from_prev = lax.ppermute(high_part, axis_name, forward)  122 us
    ppermute x34, starting transfers between devices, edge_exchange(): from_next = lax.ppermute(low_part, axis_name, backward)  113 us
    div x16, other arithmetic, cell_update(): jax.nn.sigmoid(gate_f) * c_prev + jax.nn.sigmoid(gate_i) * jnp.tanh(gate_g)  19.6 us
    squeeze x32, local copies, waits for them, and re-layouts, local_run(): lax.scan(time_step, (h_init, c_init), frames_ext)  17.5 us
    dynamic_update_slice x16, local copies, waits for them, and re-layouts, local_run(): lax.scan(time_step, (h_init, c_init), frames_ext)  17.5 us
    ppermute x34, waiting for transfers between devices, edge_exchange(): from_prev = lax.ppermute(high_part, axis_name, forward)  16.9 us
    div x32, local copies, waits for them, and re-layouts, cell_update(): jax.nn.sigmoid(gate_f) * c_prev + jax.nn.sigmoid(gate_i) * jnp.tanh(gate_g)  13.6 us
  transfers between devices with their start and end apart: 68, of which 19 were waited for; matrix products, arithmetic and copies ran while one was open for 15% of the time, Pallas kernels for 0%

commit v1 on v0

v1 whole, which is shorter than its diff:
```python
import functools

import jax
import jax.numpy as jnp
from jax import lax
from jax.experimental import pallas as pl
from jax.experimental.pallas import tpu as pltpu
from jax.sharding import PartitionSpec as P

MESH = pl.DeviceIdType.MESH
F32, BF16 = jnp.float32, jnp.bfloat16

STEPS = 16
TILE = 32
C_IN, C_HID = 64, 192
LANES = 128
PITCH = 48
ROW_SETS = (range(1, 9), range(9, 17), range(17, 25), (*range(25, 31), 0, 31))

UP, DOWN, LEFT, RIGHT = (-1, 0), (1, 0), (0, -1), (0, 1)
DIRS = (UP, DOWN, LEFT, RIGHT, (-1, -1), (-1, 1), (1, -1), (1, 1))


def sigmoid(x):
    return 0.5 * jnp.tanh(0.5 * x) + 0.5


def kernel(n_rows, n_cols, frames, w_in, w_rec, bias, h_init, c_init, hidden, c_out,
         w, lhs, st0, st1, c0, c1, ge, ce, cv, fb, ob, ci, cs, row_in, col_in, diag_in,
         send_sem, recv_sem, frame_sem, out_sem, load_sem):
    my_row, my_col = lax.axis_index("rows"), lax.axis_index("cols")

    def there(d):
        r, c = my_row + d[0], my_col + d[1]
        return (r >= 0) & (r < n_rows) & (c >= 0) & (c < n_cols)

    def device(d):
        return {"rows": my_row + d[0], "cols": my_col + d[1]}

    load_w0 = pltpu.make_async_copy(w_rec, w.at[:, 0:C_HID, :], load_sem.at[0])
    load_w1 = pltpu.make_async_copy(w_in, w.at[:, C_HID:256, :], load_sem.at[1])
    load_h = pltpu.make_async_copy(h_init, ob.at[0], load_sem.at[2])
    load_c = pltpu.make_async_copy(c_init, ci, load_sem.at[3])

    def frame_copy(t, slot):
        return pltpu.make_async_copy(frames.at[t], fb.at[slot], frame_sem.at[slot])

    def out_copy(t, slot):
        return pltpu.make_async_copy(ob.at[slot], hidden.at[t], out_sem.at[slot])

    load_h.start()
    frame_copy(0, 0).start()
    load_c.start()
    load_w0.start()
    load_w1.start()
    frame_copy(1, 1).start()

    row_in[...] = jnp.zeros_like(row_in)
    col_in[...] = jnp.zeros_like(col_in)
    diag_in[...] = jnp.zeros_like(diag_in)
    for k in range(TILE + 2):
        for st in (st0, st1):
            st[pl.ds(k * PITCH, 8), :] = jnp.zeros((8, LANES), F32)
            st[pl.ds(k * PITCH + 40, 8), :] = jnp.zeros((8, LANES), F32)

    barrier = pltpu.get_barrier_semaphore()
    for d in DIRS:
        @pl.when(there(d))
        def _():
            pl.semaphore_signal(barrier, inc=1, device_id=device(d), device_id_type=MESH)
    def near(i, n):
        return 1 + (i > 0).astype(jnp.int32) + (i < n - 1).astype(jnp.int32)

    pl.semaphore_wait(barrier, near(my_row, n_rows) * near(my_col, n_cols) - 1)

    lane = lax.broadcasted_iota(jnp.int32, (TILE, LANES), 1)
    low = lane < C_IN

    def frame_row(slot, r):
        x = fb[slot, r].astype(F32)
        return jnp.concatenate([x, x], axis=1)

    load_h.wait()
    frame_copy(0, 0).wait()
    for r in range(TILE):
        st0[pl.ds(r * PITCH + 8, TILE), :] = ob[0, r, :, 0:LANES].astype(F32)
        h1 = ob[0, r, :, LANES:C_HID].astype(F32)
        st1[pl.ds(r * PITCH + 8, TILE), :] = jnp.where(low, jnp.concatenate([h1, h1], axis=1), frame_row(0, r))
    load_c.wait()
    for r in range(TILE):
        c0[pl.ds(r * TILE, TILE), :] = ci[r, :, 0:LANES]
        v = ci[r, :, LANES:C_HID]
        c1[pl.ds(r * TILE, TILE), :] = jnp.concatenate([v, v], axis=1)
    for side in range(2):
        ce[side, 0] = c0[pl.ds((TILE - 1) * side, TILE, stride=TILE), :]
        ce[side, 1] = c1[pl.ds((TILE - 1) * side, TILE, stride=TILE), :]
    load_w0.wait()
    load_w1.wait()

    def build_row(r, out_slot):
        target = r + 1 if r < TILE else (0 if r == TILE else TILE + 1)
        for dx in range(3):
            v0 = st0[pl.ds(r * PITCH + 7 + dx, TILE), :].astype(BF16)
            v1 = st1[pl.ds(r * PITCH + 7 + dx, TILE), :].astype(BF16)
            lhs[dx, target, :, 0:LANES] = v0
            lhs[dx, target, :, LANES:256] = v1
            if dx == 1 and out_slot is not None:
                ob[out_slot, r, :, 0:LANES] = v0
                ob[out_slot, r, :, LANES:C_HID] = v1[:, 0:C_IN]

    def cell(gates, c0_prev, c1_prev):
        s0, s1, s2, s3 = (sigmoid(gates[k]) for k in range(4))
        scale = jnp.where(low, 0.5, 1.0)
        t4 = jnp.tanh(gates[4] * scale) * scale + jnp.where(low, 0.5, 0.0)
        t5 = jnp.tanh(gates[5])
        r1, r2, r4, r5 = (pltpu.roll(v, 64, 1) for v in (s1, s2, t4, t5))
        c0_next = jnp.where(low, r1, r2) * c0_prev + s0 * jnp.where(low, r4, r5)
        c1_next = r2 * c1_prev + s1 * r5
        return s3 * jnp.tanh(c0_next), t4 * jnp.tanh(c1_next), c0_next, c1_next

    def bias_piece(k):
        return bias[:, k * LANES:(k + 1) * LANES]

    def chunk_gates(rows):
        x = [jnp.concatenate([lhs[dx, r + dy] for r in rows], axis=0) for dy in range(3) for dx in range(3)]
        return jnp.dot(jnp.concatenate(x, axis=1), w[...].reshape(9 * 256, 4 * C_HID), preferred_element_type=F32)

    def cell_row(gates, j, r, x_slot):
        pre = gates[j * TILE:(j + 1) * TILE]
        pre = [pre[:, k * LANES:(k + 1) * LANES] + bias_piece(k) for k in range(6)]
        for k in range(6):
            ge[0, k, pl.ds(r * 8, 8), :] = pre[k][0:8]
            ge[1, k, pl.ds(r * 8, 8), :] = pre[k][24:32]
        at = pl.ds(r * TILE, TILE)
        h0, h1, c0_next, c1_next = cell(pre, c0[at, :], c1[at, :])
        c0[at, :] = c0_next
        c1[at, :] = c1_next
        st0[pl.ds(r * PITCH + 8, TILE), :] = h0
        st1[pl.ds(r * PITCH + 8, TILE), :] = jnp.where(low, h1, frame_row(x_slot, r))

    def sends(slot):
        pieces = (
            (UP, lhs.at[1, 1], row_in.at[slot, 1]),
            (DOWN, lhs.at[1, TILE], row_in.at[slot, 0]),
            (LEFT, cs.at[0], col_in.at[slot, 1]),
            (RIGHT, cs.at[1], col_in.at[slot, 0]),
            ((-1, -1), cs.at[0, 0:16], diag_in.at[slot, 3]),
            ((-1, 1), cs.at[1, 0:16], diag_in.at[slot, 2]),
            ((1, -1), cs.at[0, 16:32], diag_in.at[slot, 1]),
            ((1, 1), cs.at[1, 16:32], diag_in.at[slot, 0]),
        )
        return [(d, pltpu.make_async_remote_copy(
            src_ref=src, dst_ref=dst, send_sem=send_sem.at[slot, k], recv_sem=recv_sem.at[slot, k],
            device_id=device(d), device_id_type=MESH)) for k, (d, src, dst) in enumerate(pieces)]

    def wait_recv(copies, which):
        for k in which:
            d, copy = copies[k]
            @pl.when(there((-d[0], -d[1])))
            def _():
                copy.wait_recv()

    def step(t, _):
        slot = lax.rem(t, 2)
        x_slot = lax.rem(t + 1, 2)
        copies = sends(slot)

        @pl.when(t >= 3)
        def _():
            out_copy(t - 3, x_slot).wait()

        for side in range(2):
            at = pl.ds(8 + (TILE - 1) * side, TILE, stride=PITCH)
            cs[side, :, 0:LANES] = st0[at, :].astype(BF16)
            cs[side, :, LANES:256] = st1[at, :].astype(BF16)
        build_row(0, x_slot)
        build_row(TILE - 1, x_slot)
        for d, copy in copies:
            @pl.when(there(d))
            def _():
                copy.start()

        @pl.when(t < STEPS - 1)
        def _():
            frame_copy(t + 1, x_slot).wait()

        for r in range(1, 10):
            build_row(r, x_slot)
        gates = chunk_gates(ROW_SETS[0])
        for r in range(10, 18):
            build_row(r, x_slot)
        more = chunk_gates(ROW_SETS[1])
        for j, r in enumerate(ROW_SETS[0]):
            cell_row(gates, j, r, x_slot)
        for r in range(18, 31):
            build_row(r, x_slot)
        gates = chunk_gates(ROW_SETS[2])
        for j, r in enumerate(ROW_SETS[1]):
            cell_row(more, j, r, x_slot)
        for j, r in enumerate(ROW_SETS[2]):
            cell_row(gates, j, r, x_slot)

        wait_recv(copies, (0, 1))
        @pl.when(t >= 1)
        def _():
            out_copy(t - 1, x_slot).start()
        @pl.when(t < STEPS - 2)
        def _():
            frame_copy(t + 2, slot).start()
        for k in range(2):
            at = pl.ds((TILE + k) * PITCH + 8, TILE)
            st0[at, :] = row_in[slot, k, :, 0:LANES].astype(F32)
            st1[at, :] = row_in[slot, k, :, LANES:256].astype(F32)
            build_row(TILE + k, None)
        gates = chunk_gates(ROW_SETS[3])

        wait_recv(copies, range(2, 8))
        for side in range(2):
            for k in range(2):
                part = slice(k * LANES, (k + 1) * LANES)
                cv[side, k, 8:40, :] = col_in[slot, side, :, part].astype(F32)
                cv[side, k, 7:8, :] = diag_in[slot, side, 15:16, part].astype(F32)
                cv[side, k, 40:41, :] = diag_in[slot, 2 + side, 0:1, part].astype(F32)
        extra = []
        for side in range(2):
            halo = jnp.concatenate([cv[side, k, 7 + dy:39 + dy, :].astype(BF16) for dy in range(3) for k in range(2)], axis=1)
            taps = jnp.concatenate([w[dy * 3 + 2 * side] for dy in range(3)], axis=0)
            extra.append(jnp.dot(halo, taps, preferred_element_type=F32))
        for j, r in enumerate(ROW_SETS[3]):
            cell_row(gates, j, r, x_slot)
        for side in range(2):
            more = [extra[side][:, k * LANES:(k + 1) * LANES] for k in range(6)]
            pre = [ge[side, k, pl.ds(7 * side, TILE, stride=8), :] + more[k] for k in range(6)]
            h0, h1, c0_next, c1_next = cell(pre, ce[side, 0], ce[side, 1])
            ce[side, 0] = c0_next
            ce[side, 1] = c1_next
            at = pl.ds(8 + (TILE - 1) * side, TILE, stride=PITCH)
            st0[at, :] = h0
            st1[at, :] = jnp.where(low, h1, st1[at, :])
        for d, copy in copies:
            @pl.when(there(d))
            def _():
                copy.wait_send()
        return 0

    lax.fori_loop(0, STEPS, step, 0)

    out_copy(STEPS - 3, 1).wait()
    for r in range(TILE):
        at = pl.ds(r * PITCH + 8, TILE)
        ob[1, r, :, 0:LANES] = st0[at, :].astype(BF16)
        ob[1, r, :, LANES:C_HID] = st1[at, :].astype(BF16)[:, 0:C_IN]
    out_copy(STEPS - 1, 1).start()
    for side in range(2):
        c0[pl.ds((TILE - 1) * side, TILE, stride=TILE), :] = ce[side, 0]
        c1[pl.ds((TILE - 1) * side, TILE, stride=TILE), :] = ce[side, 1]
    for r in range(TILE):
        at = pl.ds(r * TILE, TILE)
        ci[r, :, 0:LANES] = c0[at, :]
        ci[r, :, LANES:C_HID] = c1[at, :][:, 0:C_IN]
    store_c = pltpu.make_async_copy(ci, c_out, load_sem.at[3])
    store_c.start()
    out_copy(STEPS - 2, 0).wait()
    out_copy(STEPS - 1, 1).wait()
    store_c.wait()


def solution(mesh):
    n_rows = mesh.shape["rows"]
    n_cols = mesh.shape["cols"]
    seq_spec = P(None, "dp", "rows", "cols", None)
    state_spec = P("dp", "rows", "cols", None)

    def local_run(frames, w_in, w_rec, gate_bias, h_init, c_init):
        frames = frames.reshape(STEPS, TILE, TILE, C_IN)
        w_in = w_in.reshape(9, C_IN, 4 * C_HID)
        w_rec = w_rec.reshape(9, C_HID, 4 * C_HID)
        bias = gate_bias.reshape(1, 4 * C_HID)
        h_init = h_init.reshape(TILE, TILE, C_HID)
        c_init = c_init.reshape(TILE, TILE, C_HID)
        hbm = pl.BlockSpec(memory_space=pltpu.HBM)
        vmem = pl.BlockSpec(memory_space=pltpu.VMEM)
        dma = pltpu.SemaphoreType.DMA
        hidden, c_last = pl.pallas_call(
            functools.partial(kernel, n_rows, n_cols),
            out_shape=(
                jax.ShapeDtypeStruct((STEPS, TILE, TILE, C_HID), BF16),
                jax.ShapeDtypeStruct((TILE, TILE, C_HID), F32),
            ),
            in_specs=[hbm, hbm, hbm, vmem, hbm, hbm],
            out_specs=(hbm, hbm),
            scratch_shapes=[
                pltpu.VMEM((9, 256, 4 * C_HID), BF16),
                pltpu.VMEM((3, TILE + 2, TILE, 256), BF16),
                pltpu.VMEM(((TILE + 2) * PITCH, LANES), F32),
                pltpu.VMEM(((TILE + 2) * PITCH, LANES), F32),
                pltpu.VMEM((TILE * TILE, LANES), F32),
                pltpu.VMEM((TILE * TILE, LANES), F32),
                pltpu.VMEM((2, 6, 8 * TILE, LANES), F32),
                pltpu.VMEM((2, 2, TILE, LANES), F32),
                pltpu.VMEM((2, 2, PITCH, LANES), F32),
                pltpu.VMEM((2, TILE, TILE, C_IN), BF16),
                pltpu.VMEM((2, TILE, TILE, C_HID), BF16),
                pltpu.VMEM((TILE, TILE, C_HID), F32),
                pltpu.VMEM((2, TILE, 256), BF16),
                pltpu.VMEM((2, 2, TILE, 256), BF16),
                pltpu.VMEM((2, 2, TILE, 256), BF16),
                pltpu.VMEM((2, 4, 16, 256), BF16),
                dma((2, 8)), dma((2, 8)), dma((2,)), dma((2,)), dma((4,)),
            ],
            compiler_params=pltpu.CompilerParams(collective_id=0, has_side_effects=True, vmem_limit_bytes=56 * 1024 * 1024),
        )(frames, w_in, w_rec, bias, h_init, c_init)
        return hidden.reshape(STEPS, 1, TILE, TILE, C_HID), c_last.reshape(1, TILE, TILE, C_HID)

    return jax.shard_map(local_run, mesh=mesh, in_specs=(seq_spec, P(), P(), P(), state_spec, state_spec), out_specs=(seq_spec, state_spec), check_vma=False)
```

time: 541 us -> 106 us (0.20); the launches traced: 534 us -> 106 us
  starting transfers between devices: 235 us -> 0 us
  matrix products: 159 us -> 0 us
  Pallas kernels: 0 us -> 94.9 us
  local copies, waits for them, and re-layouts: 70.9 us -> 10.5 us
  other arithmetic: 42.5 us -> 0 us
  waiting for transfers between devices: 22.8 us -> 0 us
    ppermute x68 -> x0, starting transfers between devices: 235 us -> none  [the longest x34 122 us: edge_exchange(): from_prev = lax.ppermute(high_part, axis_name, forward)]
    conv_general_dilated x32 -> x0, matrix products: 159 us -> none  [conv_valid(): lax.conv_general_dilated(operand, kernel, (1, 1), 'VALID', dimension_numb...]
    pallas_call x0 -> x1, Pallas kernels: none -> 94.9 us  [local_run(): pl.pallas_call(functools.partial(kernel, n_rows, n_cols), out_shape=(jax....]
    ppermute x68 -> x0, waiting for transfers between devices: 22.8 us -> none  [the longest x34 16.9 us: edge_exchange(): from_prev = lax.ppermute(high_part, axis_name, forward)]
    div x16 -> x0, other arithmetic: 19.6 us -> none  [cell_update(): jax.nn.sigmoid(gate_f) * c_prev + jax.nn.sigmoid(gate_i) * jnp.tanh(gate_g)]
    squeeze x32 -> x0, local copies, waits for them, and re-layouts: 17.5 us -> none  [local_run(): lax.scan(time_step, (h_init, c_init), frames_ext)]
    dynamic_update_slice x16 -> x0, local copies, waits for them, and re-layouts: 17.5 us -> none  [local_run(): lax.scan(time_step, (h_init, c_init), frames_ext)]
    div x32 -> x0, local copies, waits for them, and re-layouts: 13.6 us -> none  [cell_update(): jax.nn.sigmoid(gate_f) * c_prev + jax.nn.sigmoid(gate_i) * jnp.tanh(gate_g)]
  transfers between devices with their start and end apart: 68 -> 0, of which waited for: 19 -> 0; matrix products, arithmetic and copies ran while one was open for 15% -> 0% of each run, Pallas kernels for 0% -> 0%
where the time goes in v1:
time: 106 us
  Pallas kernels  94.9 us (90%)
  local copies, waits for them, and re-layouts  10.5 us (10%)
    pallas_call x1, Pallas kernels, local_run(): pl.pallas_call(functools.partial(kernel, n_rows, n_cols), out_shape=(jax....  94.9 us
    unnamed x4, local copies, waits for them, and re-layouts  9.19 us

profile of v1, /device:TPU:97, one launch (start us, length us, event | category | flops | bytes accessed | tf_op | source)
XLA Modules:
  0.0 106.0 jit_solution(15559473764730330915)
XLA Ops:
  0.6 1.3 %reshape.31.bias = f32[1,768]{1,0:T(1,128)} reshape(f32[768]{0:T(1024)} %param.9) | data formatting | bytes 6144 | tf_op jit(solution)/shard_map/reshape | solution.py:278
  1.9 94.9 %shard_map.77 = (bf16[16,32,32,192]{3,2,1,0:T(8,128)(2,1)}, f32[32,32,192]{2,1,0:T(8,128)}) custom-call(bf16[16,32,32,64]{3,2,1,0:T(8,128)(2,1)} %bitcast.10, bf16[9,64,768]{2,1,0:T(8,128)(2,1)} %bitcast.14, bf16[9,192,768]{2,1,0:T(8,128)(2,1)} %bitcast.11, f32[1,768]{1,0:T(1,128)} %reshape.31.bias, bf16[32,32,192]{2,1,0:T(8,128)(2,1)} %bitcast.15, ...), custom_call_target="tpu_custom_call" | custom-call | tf_op jit(solution)/shard_map/pallas_call | solution.py:284
  96.8 0.0 copy-start
  96.8 8.2 %copy.11 = bf16[16,1,32,32,192]{4,3,2,1,0:T(8,128)(2,1)} copy(bf16[16,1,32,32,192]{4,3,2,1,0:T(8,128)(2,1)} %bitcast.9) | data formatting | bytes 12582912
  105.0 0.0 copy-done
  105.0 1.0 copy.12
Async XLA Ops:
  96.8 8.2 %copy-start = (f32[32,32,192]{2,1,0:T(8,128)S(1)}, f32[32,32,192]{2,1,0:T(8,128)}, u32[]{:S(2)}) copy-start(f32[32,32,192]{2,1,0:T(8,128)} %get-tuple-element.5) | copy-start | bytes 2359300

commit v2 on v1

--- a/solution.py
+++ b/solution.py
@@ -26,8 +26,8 @@
 
 
 def kernel(n_rows, n_cols, frames, w_in, w_rec, bias, h_init, c_init, hidden, c_out,
-         w, lhs, st0, st1, c0, c1, ge, ce, cv, fb, ob, ci, cs, row_in, col_in, diag_in,
-         send_sem, recv_sem, frame_sem, out_sem, load_sem):
+         w, lhs, st0, st1, c0, c1, ge, ce, cv, fb, hb, bb, ci, cs, row_in, col_in, diag_in,
+         send_sem, recv_sem, frame_sem, load_sem):
     my_row, my_col = lax.axis_index("rows"), lax.axis_index("cols")
 
     def there(d):
@@ -39,16 +39,15 @@
 
     load_w0 = pltpu.make_async_copy(w_rec, w.at[:, 0:C_HID, :], load_sem.at[0])
     load_w1 = pltpu.make_async_copy(w_in, w.at[:, C_HID:256, :], load_sem.at[1])
-    load_h = pltpu.make_async_copy(h_init, ob.at[0], load_sem.at[2])
+    load_h = pltpu.make_async_copy(h_init, hb, load_sem.at[2])
     load_c = pltpu.make_async_copy(c_init, ci, load_sem.at[3])
 
     def frame_copy(t, slot):
         return pltpu.make_async_copy(frames.at[t], fb.at[slot], frame_sem.at[slot])
 
-    def out_copy(t, slot):
-        return pltpu.make_async_copy(ob.at[slot], hidden.at[t], out_sem.at[slot])
-
+    load_b = pltpu.make_async_copy(bias, bb, load_sem.at[4])
     load_h.start()
+    load_b.start()
     frame_copy(0, 0).start()
     load_c.start()
     load_w0.start()
@@ -83,9 +82,10 @@
     load_h.wait()
     frame_copy(0, 0).wait()
     for r in range(TILE):
-        st0[pl.ds(r * PITCH + 8, TILE), :] = ob[0, r, :, 0:LANES].astype(F32)
-        h1 = ob[0, r, :, LANES:C_HID].astype(F32)
+        st0[pl.ds(r * PITCH + 8, TILE), :] = hb[r, :, 0:LANES].astype(F32)
+        h1 = hb[r, :, LANES:C_HID].astype(F32)
         st1[pl.ds(r * PITCH + 8, TILE), :] = jnp.where(low, jnp.concatenate([h1, h1], axis=1), frame_row(0, r))
+    load_b.wait()
     load_c.wait()
     for r in range(TILE):
         c0[pl.ds(r * TILE, TILE), :] = ci[r, :, 0:LANES]
@@ -105,8 +105,8 @@
             lhs[dx, target, :, 0:LANES] = v0
             lhs[dx, target, :, LANES:256] = v1
             if dx == 1 and out_slot is not None:
-                ob[out_slot, r, :, 0:LANES] = v0
-                ob[out_slot, r, :, LANES:C_HID] = v1[:, 0:C_IN]
+                hidden[out_slot, r, :, 0:LANES] = v0
+                hidden[out_slot, r, :, LANES:C_HID] = v1[:, 0:C_IN]
 
     def cell(gates, c0_prev, c1_prev):
         s0, s1, s2, s3 = (sigmoid(gates[k]) for k in range(4))
@@ -119,7 +119,7 @@
         return s3 * jnp.tanh(c0_next), t4 * jnp.tanh(c1_next), c0_next, c1_next
 
     def bias_piece(k):
-        return bias[:, k * LANES:(k + 1) * LANES]
+        return bb[k * LANES:(k + 1) * LANES].reshape(1, LANES)
 
     def chunk_gates(rows):
         x = [jnp.concatenate([lhs[dx, r + dy] for r in rows], axis=0) for dy in range(3) for dx in range(3)]
@@ -165,16 +165,13 @@
         x_slot = lax.rem(t + 1, 2)
         copies = sends(slot)
 
-        @pl.when(t >= 3)
-        def _():
-            out_copy(t - 3, x_slot).wait()
-
+        done = lax.rem(t + STEPS - 1, STEPS)
         for side in range(2):
             at = pl.ds(8 + (TILE - 1) * side, TILE, stride=PITCH)
             cs[side, :, 0:LANES] = st0[at, :].astype(BF16)
             cs[side, :, LANES:256] = st1[at, :].astype(BF16)
-        build_row(0, x_slot)
-        build_row(TILE - 1, x_slot)
+        build_row(0, done)
+        build_row(TILE - 1, done)
         for d, copy in copies:
             @pl.when(there(d))
             def _():
@@ -185,25 +182,19 @@
             frame_copy(t + 1, x_slot).wait()
 
         for r in range(1, 10):
-            build_row(r, x_slot)
+            build_row(r, done)
         gates = chunk_gates(ROW_SETS[0])
         for r in range(10, 18):
-            build_row(r, x_slot)
+            build_row(r, done)
         more = chunk_gates(ROW_SETS[1])
         for j, r in enumerate(ROW_SETS[0]):
             cell_row(gates, j, r, x_slot)
         for r in range(18, 31):
-            build_row(r, x_slot)
+            build_row(r, done)
         gates = chunk_gates(ROW_SETS[2])
         for j, r in enumerate(ROW_SETS[1]):
             cell_row(more, j, r, x_slot)
-        for j, r in enumerate(ROW_SETS[2]):
-            cell_row(gates, j, r, x_slot)
-
         wait_recv(copies, (0, 1))
-        @pl.when(t >= 1)
-        def _():
-            out_copy(t - 1, x_slot).start()
         @pl.when(t < STEPS - 2)
         def _():
             frame_copy(t + 2, slot).start()
@@ -212,7 +203,9 @@
             st0[at, :] = row_in[slot, k, :, 0:LANES].astype(F32)
             st1[at, :] = row_in[slot, k, :, LANES:256].astype(F32)
             build_row(TILE + k, None)
-        gates = chunk_gates(ROW_SETS[3])
+        more = chunk_gates(ROW_SETS[3])
+        for j, r in enumerate(ROW_SETS[2]):
+            cell_row(gates, j, r, x_slot)
 
         wait_recv(copies, range(2, 8))
         for side in range(2):
@@ -227,7 +220,7 @@
             taps = jnp.concatenate([w[dy * 3 + 2 * side] for dy in range(3)], axis=0)
             extra.append(jnp.dot(halo, taps, preferred_element_type=F32))
         for j, r in enumerate(ROW_SETS[3]):
-            cell_row(gates, j, r, x_slot)
+            cell_row(more, j, r, x_slot)
         for side in range(2):
             more = [extra[side][:, k * LANES:(k + 1) * LANES] for k in range(6)]
             pre = [ge[side, k, pl.ds(7 * side, TILE, stride=8), :] + more[k] for k in range(6)]
@@ -245,24 +238,17 @@
 
     lax.fori_loop(0, STEPS, step, 0)
 
-    out_copy(STEPS - 3, 1).wait()
     for r in range(TILE):
         at = pl.ds(r * PITCH + 8, TILE)
-        ob[1, r, :, 0:LANES] = st0[at, :].astype(BF16)
-        ob[1, r, :, LANES:C_HID] = st1[at, :].astype(BF16)[:, 0:C_IN]
-    out_copy(STEPS - 1, 1).start()
+        hidden[STEPS - 1, r, :, 0:LANES] = st0[at, :].astype(BF16)
+        hidden[STEPS - 1, r, :, LANES:C_HID] = st1[at, :].astype(BF16)[:, 0:C_IN]
     for side in range(2):
         c0[pl.ds((TILE - 1) * side, TILE, stride=TILE), :] = ce[side, 0]
         c1[pl.ds((TILE - 1) * side, TILE, stride=TILE), :] = ce[side, 1]
     for r in range(TILE):
         at = pl.ds(r * TILE, TILE)
-        ci[r, :, 0:LANES] = c0[at, :]
-        ci[r, :, LANES:C_HID] = c1[at, :][:, 0:C_IN]
-    store_c = pltpu.make_async_copy(ci, c_out, load_sem.at[3])
-    store_c.start()
-    out_copy(STEPS - 2, 0).wait()
-    out_copy(STEPS - 1, 1).wait()
-    store_c.wait()
+        c_out[r, :, 0:LANES] = c0[at, :]
+        c_out[r, :, LANES:C_HID] = c1[at, :][:, 0:C_IN]
 
 
 def solution(mesh):
@@ -275,7 +261,6 @@
         frames = frames.reshape(STEPS, TILE, TILE, C_IN)
         w_in = w_in.reshape(9, C_IN, 4 * C_HID)
         w_rec = w_rec.reshape(9, C_HID, 4 * C_HID)
-        bias = gate_bias.reshape(1, 4 * C_HID)
         h_init = h_init.reshape(TILE, TILE, C_HID)
         c_init = c_init.reshape(TILE, TILE, C_HID)
         hbm = pl.BlockSpec(memory_space=pltpu.HBM)
@@ -284,11 +269,11 @@
         hidden, c_last = pl.pallas_call(
             functools.partial(kernel, n_rows, n_cols),
             out_shape=(
-                jax.ShapeDtypeStruct((STEPS, TILE, TILE, C_HID), BF16),
-                jax.ShapeDtypeStruct((TILE, TILE, C_HID), F32),
+                pltpu.VMEM((STEPS, TILE, TILE, C_HID), BF16),
+                pltpu.VMEM((TILE, TILE, C_HID), F32),
             ),
-            in_specs=[hbm, hbm, hbm, vmem, hbm, hbm],
-            out_specs=(hbm, hbm),
+            in_specs=[hbm] * 6,
+            out_specs=(vmem, vmem),
             scratch_shapes=[
                 pltpu.VMEM((9, 256, 4 * C_HID), BF16),
                 pltpu.VMEM((3, TILE + 2, TILE, 256), BF16),
@@ -300,16 +285,17 @@
                 pltpu.VMEM((2, 2, TILE, LANES), F32),
                 pltpu.VMEM((2, 2, PITCH, LANES), F32),
                 pltpu.VMEM((2, TILE, TILE, C_IN), BF16),
-                pltpu.VMEM((2, TILE, TILE, C_HID), BF16),
+                pltpu.VMEM((TILE, TILE, C_HID), BF16),
+                pltpu.VMEM((4 * C_HID,), F32),
                 pltpu.VMEM((TILE, TILE, C_HID), F32),
                 pltpu.VMEM((2, TILE, 256), BF16),
                 pltpu.VMEM((2, 2, TILE, 256), BF16),
                 pltpu.VMEM((2, 2, TILE, 256), BF16),
                 pltpu.VMEM((2, 4, 16, 256), BF16),
-                dma((2, 8)), dma((2, 8)), dma((2,)), dma((2,)), dma((4,)),
+                dma((2, 8)), dma((2, 8)), dma((2,)), dma((5,)),
             ],
-            compiler_params=pltpu.CompilerParams(collective_id=0, has_side_effects=True, vmem_limit_bytes=56 * 1024 * 1024),
-        )(frames, w_in, w_rec, bias, h_init, c_init)
+            compiler_params=pltpu.CompilerParams(collective_id=0, has_side_effects=True, vmem_limit_bytes=52 * 1024 * 1024),
+        )(frames, w_in, w_rec, gate_bias, h_init, c_init)
         return hidden.reshape(STEPS, 1, TILE, TILE, C_HID), c_last.reshape(1, TILE, TILE, C_HID)
 
     return jax.shard_map(local_run, mesh=mesh, in_specs=(seq_spec, P(), P(), P(), state_spec, state_spec), out_specs=(seq_spec, state_spec), check_vma=False)

time: 106 us -> 96.5 us (0.910)
  local copies, waits for them, and re-layouts: 10.5 us -> 4.37 us
  Pallas kernels: 94.9 us -> 91.4 us
    unnamed x4 -> x2, local copies, waits for them, and re-layouts: 9.19 us -> 4.37 us
    pallas_call x1, Pallas kernels: 94.9 us -> 91.4 us  [local_run(): pl.pallas_call(functools.partial(kernel, n_rows, n_cols), out_shape=(pltp...]
    reshape x1 -> x0, local copies, waits for them, and re-layouts: 1.27 us -> none  [local_run(): bias = gate_bias.reshape(1, 4 * C_HID)]
where the time goes in v2:
time: 96.5 us; the launch traced here: 96.4 us
  Pallas kernels  91.4 us (95%)
  local copies, waits for them, and re-layouts  4.37 us (5%)
    pallas_call x1, Pallas kernels, local_run(): pl.pallas_call(functools.partial(kernel, n_rows, n_cols), out_shape=(pltp...  91.4 us
    unnamed x2, local copies, waits for them, and re-layouts  4.37 us

profile of v2, /device:TPU:97, one launch (start us, length us, event | category | flops | bytes accessed | tf_op | source)
XLA Modules:
  0.0 96.4 jit_solution(4635991637020837384)
XLA Ops:
  0.6 91.4 %shard_map.77 = (bf16[16,32,32,192]{3,2,1,0:T(8,128)(2,1)S(1)}, f32[32,32,192]{2,1,0:T(8,128)S(1)}) custom-call(bf16[16,32,32,64]{3,2,1,0:T(8,128)(2,1)} %bitcast.11, bf16[9,64,768]{2,1,0:T(8,128)(2,1)} %bitcast.14, bf16[9,192,768]{2,1,0:T(8,128)(2,1)} %bitcast.12, f32[768]{0:T(1024)} %bias.1, bf16[32,32,192]{2,1,0:T(8,128)(2,1)} %bitcast.15, ...), custom_call_target="tpu_custom_call" | custom-call | tf_op jit(solution)/shard_map/pallas_call | solution.py:269
  92.0 3.4 %copy.11 = bf16[16,1,32,32,192]{4,3,2,1,0:T(8,128)(2,1)} copy(bf16[16,1,32,32,192]{4,3,2,1,0:T(8,128)(2,1)S(1)} %bitcast.9) | data formatting | bytes 12582912
  95.4 1.0 %copy.12 = f32[1,32,32,192]{3,2,1,0:T(8,128)} copy(f32[1,32,32,192]{3,2,1,0:T(8,128)S(1)} %bitcast.10) | data formatting | bytes 1572864

commit v3 on v2

--- a/solution.py
+++ b/solution.py
@@ -16,6 +16,8 @@
 LANES = 128
 PITCH = 48
 ROW_SETS = (range(1, 9), range(9, 17), range(17, 25), (*range(25, 31), 0, 31))
+HALVES = (2, 2, 2, 2)
+LATE = 6
 
 UP, DOWN, LEFT, RIGHT = (-1, 0), (1, 0), (0, -1), (0, 1)
 DIRS = (UP, DOWN, LEFT, RIGHT, (-1, -1), (-1, 1), (1, -1), (1, 1))
@@ -26,7 +28,7 @@
 
 
 def kernel(n_rows, n_cols, frames, w_in, w_rec, bias, h_init, c_init, hidden, c_out,
-         w, lhs, st0, st1, c0, c1, ge, ce, cv, fb, hb, bb, ci, cs, row_in, col_in, diag_in,
+         w, lhs, st0, st1, c0, c1, ge, gp, ce, cv, fb, hb, bb, ci, cs, row_in, col_in, diag_in,
          send_sem, recv_sem, frame_sem, load_sem):
     my_row, my_col = lax.axis_index("rows"), lax.axis_index("cols")
 
@@ -57,6 +59,7 @@
     row_in[...] = jnp.zeros_like(row_in)
     col_in[...] = jnp.zeros_like(col_in)
     diag_in[...] = jnp.zeros_like(diag_in)
+    gp[...] = jnp.zeros_like(gp)
     for k in range(TILE + 2):
         for st in (st0, st1):
             st[pl.ds(k * PITCH, 8), :] = jnp.zeros((8, LANES), F32)
@@ -74,6 +77,7 @@
 
     lane = lax.broadcasted_iota(jnp.int32, (TILE, LANES), 1)
     low = lane < C_IN
+    cell_at = lax.broadcasted_iota(jnp.int32, (TILE, LANES), 0)
 
     def frame_row(slot, r):
         x = fb[slot, r].astype(F32)
@@ -94,16 +98,18 @@
     for side in range(2):
         ce[side, 0] = c0[pl.ds((TILE - 1) * side, TILE, stride=TILE), :]
         ce[side, 1] = c1[pl.ds((TILE - 1) * side, TILE, stride=TILE), :]
-    load_w0.wait()
-    load_w1.wait()
+        at = pl.ds(8 + (TILE - 1) * side, TILE, stride=PITCH)
+        cs[side, :, 0:LANES] = st0[at, :].astype(BF16)
+        cs[side, :, LANES:256] = st1[at, :].astype(BF16)
 
     def build_row(r, out_slot):
         target = r + 1 if r < TILE else (0 if r == TILE else TILE + 1)
         for dx in range(3):
             v0 = st0[pl.ds(r * PITCH + 7 + dx, TILE), :].astype(BF16)
             v1 = st1[pl.ds(r * PITCH + 7 + dx, TILE), :].astype(BF16)
-            lhs[dx, target, :, 0:LANES] = v0
-            lhs[dx, target, :, LANES:256] = v1
+            if dx != 1 or r not in (0, TILE - 1):
+                lhs[dx, target, :, 0:LANES] = v0
+                lhs[dx, target, :, LANES:256] = v1
             if dx == 1 and out_slot is not None:
                 hidden[out_slot, r, :, 0:LANES] = v0
                 hidden[out_slot, r, :, LANES:C_HID] = v1[:, 0:C_IN]
@@ -121,22 +127,42 @@
     def bias_piece(k):
         return bb[k * LANES:(k + 1) * LANES].reshape(1, LANES)
 
-    def chunk_gates(rows):
+    def chunk_gates(rows, halves):
         x = [jnp.concatenate([lhs[dx, r + dy] for r in rows], axis=0) for dy in range(3) for dx in range(3)]
-        return jnp.dot(jnp.concatenate(x, axis=1), w[...].reshape(9 * 256, 4 * C_HID), preferred_element_type=F32)
-
-    def cell_row(gates, j, r, x_slot):
-        pre = gates[j * TILE:(j + 1) * TILE]
+        x = jnp.concatenate(x, axis=1)
+        weights = w[...].reshape(9 * 256, 4 * C_HID)
+        wide = jnp.dot(x, weights[:, 0:512], preferred_element_type=F32)
+        size = x.shape[0] // halves
+        rest = [jnp.dot(x[k * size:(k + 1) * size], weights[:, 512:], preferred_element_type=F32) for k in range(halves)]
+        return wide, jnp.concatenate(rest, axis=0)
+
+    def gate_row(gates, j, r):
+        pre = jnp.concatenate([g[j * TILE:(j + 1) * TILE] for g in gates], axis=1)
         pre = [pre[:, k * LANES:(k + 1) * LANES] + bias_piece(k) for k in range(6)]
         for k in range(6):
             ge[0, k, pl.ds(r * 8, 8), :] = pre[k][0:8]
             ge[1, k, pl.ds(r * 8, 8), :] = pre[k][24:32]
+        return pre
+
+    def cell_row(gates, j, r, x_slot):
+        pre = gate_row(gates, j, r)
         at = pl.ds(r * TILE, TILE)
         h0, h1, c0_next, c1_next = cell(pre, c0[at, :], c1[at, :])
         c0[at, :] = c0_next
         c1[at, :] = c1_next
         st0[pl.ds(r * PITCH + 8, TILE), :] = h0
         st1[pl.ds(r * PITCH + 8, TILE), :] = jnp.where(low, h1, frame_row(x_slot, r))
+
+    def cell_row_late(j, r, t):
+        at = pl.ds(r * TILE, TILE)
+        here = pl.ds(r * PITCH + 8, TILE)
+        live = jnp.full((TILE, LANES), t, jnp.int32) > 0
+        inner = live & (cell_at > 0) & (cell_at < TILE - 1)
+        h0, h1, c0_next, c1_next = cell([gp[j, k] for k in range(6)], c0[at, :], c1[at, :])
+        c0[at, :] = jnp.where(live, c0_next, c0[at, :])
+        c1[at, :] = jnp.where(live, c1_next, c1[at, :])
+        st0[here, :] = jnp.where(inner, h0, st0[here, :])
+        st1[here, :] = jnp.where(inner & low, h1, st1[here, :])
 
     def sends(slot):
         pieces = (
@@ -166,12 +192,10 @@
         copies = sends(slot)
 
         done = lax.rem(t + STEPS - 1, STEPS)
-        for side in range(2):
-            at = pl.ds(8 + (TILE - 1) * side, TILE, stride=PITCH)
-            cs[side, :, 0:LANES] = st0[at, :].astype(BF16)
-            cs[side, :, LANES:256] = st1[at, :].astype(BF16)
-        build_row(0, done)
-        build_row(TILE - 1, done)
+        for r in (0, TILE - 1):
+            here = pl.ds(r * PITCH + 8, TILE)
+            lhs[1, r + 1, :, 0:LANES] = st0[here, :].astype(BF16)
+            lhs[1, r + 1, :, LANES:256] = st1[here, :].astype(BF16)
         for d, copy in copies:
             @pl.when(there(d))
             def _():
@@ -181,19 +205,29 @@
         def _():
             frame_copy(t + 1, x_slot).wait()
 
-        for r in range(1, 10):
+        @pl.when(t == 0)
+        def _():
+            load_w0.wait()
+            load_w1.wait()
+
+        built = 0
+        before = None
+        for i, rows in enumerate(ROW_SETS[:-1]):
+            top = min(max(rows) + 2, TILE)
+            for r in range(built, top):
+                build_row(r, done)
+            built = top
+            gates = chunk_gates(rows, HALVES[i])
+            if i == 0:
+                for j in range(LATE):
+                    cell_row_late(j, ROW_SETS[-1][j], t)
+            if before is not None:
+                for j, r in enumerate(ROW_SETS[i - 1]):
+                    cell_row(before, j, r, x_slot)
+            before = gates
+        for r in range(built, TILE):
             build_row(r, done)
-        gates = chunk_gates(ROW_SETS[0])
-        for r in range(10, 18):
-            build_row(r, done)
-        more = chunk_gates(ROW_SETS[1])
-        for j, r in enumerate(ROW_SETS[0]):
-            cell_row(gates, j, r, x_slot)
-        for r in range(18, 31):
-            build_row(r, done)
-        gates = chunk_gates(ROW_SETS[2])
-        for j, r in enumerate(ROW_SETS[1]):
-            cell_row(more, j, r, x_slot)
+
         wait_recv(copies, (0, 1))
         @pl.when(t < STEPS - 2)
         def _():
@@ -203,11 +237,15 @@
             st0[at, :] = row_in[slot, k, :, 0:LANES].astype(F32)
             st1[at, :] = row_in[slot, k, :, LANES:256].astype(F32)
             build_row(TILE + k, None)
-        more = chunk_gates(ROW_SETS[3])
-        for j, r in enumerate(ROW_SETS[2]):
-            cell_row(gates, j, r, x_slot)
+        more = chunk_gates(ROW_SETS[-1], HALVES[-1])
+        for j, r in enumerate(ROW_SETS[-2]):
+            cell_row(before, j, r, x_slot)
 
         wait_recv(copies, range(2, 8))
+        for d, copy in copies:
+            @pl.when(there(d))
+            def _():
+                copy.wait_send()
         for side in range(2):
             for k in range(2):
                 part = slice(k * LANES, (k + 1) * LANES)
@@ -219,8 +257,13 @@
             halo = jnp.concatenate([cv[side, k, 7 + dy:39 + dy, :].astype(BF16) for dy in range(3) for k in range(2)], axis=1)
             taps = jnp.concatenate([w[dy * 3 + 2 * side] for dy in range(3)], axis=0)
             extra.append(jnp.dot(halo, taps, preferred_element_type=F32))
-        for j, r in enumerate(ROW_SETS[3]):
-            cell_row(more, j, r, x_slot)
+        for j, r in enumerate(ROW_SETS[-1]):
+            if j < LATE:
+                for k, v in enumerate(gate_row(more, j, r)):
+                    gp[j, k] = v
+                st1[pl.ds(r * PITCH + 8, TILE), :] = frame_row(x_slot, r)
+            else:
+                cell_row(more, j, r, x_slot)
         for side in range(2):
             more = [extra[side][:, k * LANES:(k + 1) * LANES] for k in range(6)]
             pre = [ge[side, k, pl.ds(7 * side, TILE, stride=8), :] + more[k] for k in range(6)]
@@ -228,16 +271,17 @@
             ce[side, 0] = c0_next
             ce[side, 1] = c1_next
             at = pl.ds(8 + (TILE - 1) * side, TILE, stride=PITCH)
+            h1 = jnp.where(low, h1, st1[at, :])
             st0[at, :] = h0
-            st1[at, :] = jnp.where(low, h1, st1[at, :])
-        for d, copy in copies:
-            @pl.when(there(d))
-            def _():
-                copy.wait_send()
+            st1[at, :] = h1
+            cs[side, :, 0:LANES] = h0.astype(BF16)
+            cs[side, :, LANES:256] = h1.astype(BF16)
         return 0
 
     lax.fori_loop(0, STEPS, step, 0)
 
+    for j in range(LATE):
+        cell_row_late(j, ROW_SETS[-1][j], STEPS)
     for r in range(TILE):
         at = pl.ds(r * PITCH + 8, TILE)
         hidden[STEPS - 1, r, :, 0:LANES] = st0[at, :].astype(BF16)
@@ -249,6 +293,15 @@
         at = pl.ds(r * TILE, TILE)
         c_out[r, :, 0:LANES] = c0[at, :]
         c_out[r, :, LANES:C_HID] = c1[at, :][:, 0:C_IN]
+
+
+def store_kernel(hidden, c_last, hidden_out, c_out, sem):
+    copies = [pltpu.make_async_copy(c_last, c_out, sem.at[STEPS])]
+    copies += [pltpu.make_async_copy(hidden.at[t], hidden_out.at[t], sem.at[t]) for t in range(STEPS)]
+    for copy in copies:
+        copy.start()
+    for copy in copies:
+        copy.wait()
 
 
 def solution(mesh):
@@ -282,6 +335,7 @@
                 pltpu.VMEM((TILE * TILE, LANES), F32),
                 pltpu.VMEM((TILE * TILE, LANES), F32),
                 pltpu.VMEM((2, 6, 8 * TILE, LANES), F32),
+                pltpu.VMEM((LATE, 6, TILE, LANES), F32),
                 pltpu.VMEM((2, 2, TILE, LANES), F32),
                 pltpu.VMEM((2, 2, PITCH, LANES), F32),
                 pltpu.VMEM((2, TILE, TILE, C_IN), BF16),
@@ -296,6 +350,19 @@
             ],
             compiler_params=pltpu.CompilerParams(collective_id=0, has_side_effects=True, vmem_limit_bytes=52 * 1024 * 1024),
         )(frames, w_in, w_rec, gate_bias, h_init, c_init)
+        hidden = pltpu.with_memory_space_constraint(hidden, pltpu.VMEM)
+        c_last = pltpu.with_memory_space_constraint(c_last, pltpu.VMEM)
+        hidden, c_last = pl.pallas_call(
+            store_kernel,
+            out_shape=(
+                jax.ShapeDtypeStruct((STEPS, TILE, TILE, C_HID), BF16),
+                jax.ShapeDtypeStruct((TILE, TILE, C_HID), F32),
+            ),
+            in_specs=[vmem, vmem],
+            out_specs=(hbm, hbm),
+            scratch_shapes=[dma((STEPS + 1,))],
+            compiler_params=pltpu.CompilerParams(vmem_limit_bytes=1024 * 1024),
+        )(hidden, c_last)
         return hidden.reshape(STEPS, 1, TILE, TILE, C_HID), c_last.reshape(1, TILE, TILE, C_HID)
 
     return jax.shard_map(local_run, mesh=mesh, in_specs=(seq_spec, P(), P(), P(), state_spec, state_spec), out_specs=(seq_spec, state_spec), check_vma=False)

time: 96.5 us -> 86.7 us (0.90)
  Pallas kernels: 91.4 us -> 85.9 us
  local copies, waits for them, and re-layouts: 4.37 us -> 0 us
    pallas_call x1, Pallas kernels: 91.4 us -> 82.2 us  [local_run(): pl.pallas_call(functools.partial(kernel, n_rows, n_cols), out_shape=(pltp...]
    unnamed x2 -> x0, local copies, waits for them, and re-layouts: 4.37 us -> none
    pallas_call x0 -> x1, Pallas kernels: none -> 3.74 us  [local_run(): pl.pallas_call(store_kernel, out_shape=(jax.ShapeDtypeStruct((STEPS, TILE...]
where the time goes in v3:
time: 86.7 us; the launch traced here: 86.6 us
  Pallas kernels  85.9 us (99%)
    pallas_call x1, Pallas kernels, local_run(): pl.pallas_call(functools.partial(kernel, n_rows, n_cols), out_shape=(pltp...  82.2 us
    pallas_call x1, Pallas kernels, local_run(): pl.pallas_call(store_kernel, out_shape=(jax.ShapeDtypeStruct((STEPS, TILE...  3.74 us

profile of v3, /device:TPU:97, one launch (start us, length us, event | category | flops | bytes accessed | tf_op | source)
XLA Modules:
  0.0 86.6 jit_solution(843036363218178952)
XLA Ops:
  0.6 82.2 %shard_map.77 = (bf16[16,32,32,192]{3,2,1,0:T(8,128)(2,1)S(1)}, f32[32,32,192]{2,1,0:T(8,128)S(1)}) custom-call(bf16[16,32,32,64]{3,2,1,0:T(8,128)(2,1)} %bitcast.9, bf16[9,64,768]{2,1,0:T(8,128)(2,1)} %bitcast.12, bf16[9,192,768]{2,1,0:T(8,128)(2,1)} %bitcast.10, f32[768]{0:T(1024)} %bias.1, bf16[32,32,192]{2,1,0:T(8,128)(2,1)} %bitcast.13, ...), custom_call_target="tpu_custom_call" | custom-call | tf_op jit(solution)/shard_map/pallas_call | solution.py:322
  82.8 3.7 %shard_map.78 = (bf16[16,32,32,192]{3,2,1,0:T(8,128)(2,1)}, f32[32,32,192]{2,1,0:T(8,128)}) custom-call(bf16[16,32,32,192]{3,2,1,0:T(8,128)(2,1)S(1)} %get-tuple-element.6.hidden, f32[32,32,192]{2,1,0:T(8,128)S(1)} %get-tuple-element.7.c_last), custom_call_target="tpu_custom_call" | custom-call | tf_op jit(solution)/shard_map/pallas_call | solution.py:355

commit v4 on v3

--- a/solution.py
+++ b/solution.py
@@ -17,6 +17,8 @@
 PITCH = 48
 ROW_SETS = (range(1, 9), range(9, 17), range(17, 25), (*range(25, 31), 0, 31))
 HALVES = (2, 2, 2, 2)
+SPLIT3 = 8
+SPLIT4 = 8
 LATE = 6
 
 UP, DOWN, LEFT, RIGHT = (-1, 0), (1, 0), (0, -1), (0, 1)
@@ -127,14 +129,19 @@
     def bias_piece(k):
         return bb[k * LANES:(k + 1) * LANES].reshape(1, LANES)
 
-    def chunk_gates(rows, halves):
-        x = [jnp.concatenate([lhs[dx, r + dy] for r in rows], axis=0) for dy in range(3) for dx in range(3)]
+    def products(rows, halves, taps):
+        x = [jnp.concatenate([lhs[tap % 3, r + tap // 3] for r in rows], axis=0) for tap in taps]
         x = jnp.concatenate(x, axis=1)
-        weights = w[...].reshape(9 * 256, 4 * C_HID)
-        wide = jnp.dot(x, weights[:, 0:512], preferred_element_type=F32)
+        weights = w[taps[0]:taps[-1] + 1].reshape(len(taps) * 256, 4 * C_HID)
         size = x.shape[0] // halves
         rest = [jnp.dot(x[k * size:(k + 1) * size], weights[:, 512:], preferred_element_type=F32) for k in range(halves)]
-        return wide, jnp.concatenate(rest, axis=0)
+        return [jnp.dot(x, weights[:, 0:512], preferred_element_type=F32)] + rest
+
+    def whole(parts):
+        return parts[0], jnp.concatenate(parts[1:], axis=0)
+
+    def chunk_gates(rows, halves):
+        return whole(products(rows, halves, range(9)))
 
     def gate_row(gates, j, r):
         pre = jnp.concatenate([g[j * TILE:(j + 1) * TILE] for g in gates], axis=1)
@@ -201,6 +208,9 @@
             def _():
                 copy.start()
 
+        @pl.when(t < STEPS - 2)
+        def _():
+            frame_copy(t + 2, slot).start()
         @pl.when(t < STEPS - 1)
         def _():
             frame_copy(t + 1, x_slot).wait()
@@ -217,7 +227,10 @@
             for r in range(built, top):
                 build_row(r, done)
             built = top
-            gates = chunk_gates(rows, HALVES[i])
+            if i < len(ROW_SETS) - 2:
+                gates = chunk_gates(rows, HALVES[i])
+            else:
+                gates = products(rows, HALVES[i], range(SPLIT3))
             if i == 0:
                 for j in range(LATE):
                     cell_row_late(j, ROW_SETS[-1][j], t)
@@ -229,15 +242,14 @@
             build_row(r, done)
 
         wait_recv(copies, (0, 1))
-        @pl.when(t < STEPS - 2)
-        def _():
-            frame_copy(t + 2, slot).start()
+        rest = products(ROW_SETS[-2], HALVES[-2], range(SPLIT3, 9))
+        before = whole([b + a for a, b in zip(before, rest)])
         for k in range(2):
             at = pl.ds((TILE + k) * PITCH + 8, TILE)
             st0[at, :] = row_in[slot, k, :, 0:LANES].astype(F32)
             st1[at, :] = row_in[slot, k, :, LANES:256].astype(F32)
             build_row(TILE + k, None)
-        more = chunk_gates(ROW_SETS[-1], HALVES[-1])
+        more = products(ROW_SETS[-1], HALVES[-1], range(SPLIT4))
         for j, r in enumerate(ROW_SETS[-2]):
             cell_row(before, j, r, x_slot)
 
@@ -246,6 +258,8 @@
             @pl.when(there(d))
             def _():
                 copy.wait_send()
+        rest = products(ROW_SETS[-1], HALVES[-1], range(SPLIT4, 9))
+        more = whole([b + a for a, b in zip(more, rest)])
         for side in range(2):
             for k in range(2):
                 part = slice(k * LANES, (k + 1) * LANES)

time: 86.7 us -> 86.5 us (level)
  no operation moved by 1% of the time
where the time goes in v4:
time: 86.5 us; the launch traced here: 86.4 us
  Pallas kernels  85.8 us (99%)
    pallas_call x1, Pallas kernels, local_run(): pl.pallas_call(functools.partial(kernel, n_rows, n_cols), out_shape=(pltp...  82 us
    pallas_call x1, Pallas kernels, local_run(): pl.pallas_call(store_kernel, out_shape=(jax.ShapeDtypeStruct((STEPS, TILE...  3.74 us

profile of v4, /device:TPU:97, one launch (start us, length us, event | category | flops | bytes accessed | tf_op | source)
XLA Modules:
  0.0 86.4 jit_solution(10462321810215813768)
XLA Ops:
  0.6 82.0 %shard_map.77 = (bf16[16,32,32,192]{3,2,1,0:T(8,128)(2,1)S(1)}, f32[32,32,192]{2,1,0:T(8,128)S(1)}) custom-call(bf16[16,32,32,64]{3,2,1,0:T(8,128)(2,1)} %bitcast.9, bf16[9,64,768]{2,1,0:T(8,128)(2,1)} %bitcast.12, bf16[9,192,768]{2,1,0:T(8,128)(2,1)} %bitcast.10, f32[768]{0:T(1024)} %bias.1, bf16[32,32,192]{2,1,0:T(8,128)(2,1)} %bitcast.13, ...), custom_call_target="tpu_custom_call" | custom-call | tf_op jit(solution)/shard_map/pallas_call | solution.py:336
  82.7 3.7 %shard_map.78 = (bf16[16,32,32,192]{3,2,1,0:T(8,128)(2,1)}, f32[32,32,192]{2,1,0:T(8,128)}) custom-call(bf16[16,32,32,192]{3,2,1,0:T(8,128)(2,1)S(1)} %get-tuple-element.6.hidden, f32[32,32,192]{2,1,0:T(8,128)S(1)} %get-tuple-element.7.c_last), custom_call_target="tpu_custom_call" | custom-call | tf_op jit(solution)/shard_map/pallas_call | solution.py:369
